TPU v7x, 32 devices: a whole 2x2x4 slice. The times are simulated.
32 devices in a mesh: fsdp: 16 (over z, x, core), tensor: 2 (over y).
Axes of the slice: x: 2, y: 2, z: 4, core: 2. Of those that a mesh axis runs over, the one named last changes fastest.
Arguments:
- tokens: bfloat16 [6144, 2048], P(('fsdp', 'tensor')), may hold values from -6 to 6
- segment_ids: int32 [16, 384], P('fsdp'), may hold values from 0 to 2, never falling along the last dimension, each value on 1 to 192 neighbouring positions
- w_query: bfloat16 [2048, 2048], P('fsdp', 'tensor'), may hold values from -0.125 to 0.125
- w_key: bfloat16 [2048, 2048], P('fsdp', 'tensor'), may hold values from -0.125 to 0.125
- w_value: bfloat16 [2048, 2048], P('fsdp', 'tensor'), may hold values from -0.125 to 0.125
- w_out: bfloat16 [2048, 2048], P('tensor', 'fsdp'), may hold values from -0.125 to 0.125
- w_gate: bfloat16 [2048, 8192], P('fsdp', 'tensor'), may hold values from -0.125 to 0.125
- w_up: bfloat16 [2048, 8192], P('fsdp', 'tensor'), may hold values from -0.125 to 0.125
- w_down: bfloat16 [8192, 2048], P('tensor', 'fsdp'), may hold values from -0.0625 to 0.0625
- gain_query: bfloat16 [2048], P('fsdp'), may hold values from 0.25 to 1.75
- gain_key: bfloat16 [2048], P('fsdp'), may hold values from 0.25 to 1.75
- gain_attn: bfloat16 [2048], P('fsdp'), may hold values from 0.25 to 1.75
- gain_ffn: bfloat16 [2048], P('fsdp'), may hold values from 0.25 to 1.75
- cotangent: bfloat16 [6144, 2048], P(('fsdp', 'tensor')), may hold values from -6 to 6
Outputs:
- layer_out: bfloat16 [6144, 2048], P(('fsdp', 'tensor'))
- grad_tokens: float32 [6144, 2048], P(('fsdp', 'tensor'))
- grad_w_query: float32 [2048, 2048], P('fsdp', 'tensor')
- grad_w_key: float32 [2048, 2048], P('fsdp', 'tensor')
- grad_w_value: float32 [2048, 2048], P('fsdp', 'tensor')
- grad_w_out: float32 [2048, 2048], P('tensor', 'fsdp')
- grad_w_gate: float32 [2048, 8192], P('fsdp', 'tensor')
- grad_w_up: float32 [2048, 8192], P('fsdp', 'tensor')
- grad_w_down: float32 [8192, 2048], P('tensor', 'fsdp')
- grad_gain_query: float32 [2048], P('fsdp')
- grad_gain_key: float32 [2048], P('fsdp')
- grad_gain_attn: float32 [2048], P('fsdp')
- grad_gain_ffn: float32 [2048], P('fsdp')
Inputs may be any that keep to these rules, and one draw needn't show every extreme that they name: `segment_ids`: in each row, ids never fall; each of the 3 ids covers 1 to 192 positions, and one covers exactly 192.
All inputs are finite; a program needn't handle non-finite values.
Results may differ from a plain program's by a relative error of at most 0.015.
Values may be sent and summed in bfloat16 or wider, within the bound.
A program may use at most 256 MiB of HBM per device.

v0:
```python
import jax
import jax.numpy as jnp
from jax import lax
from jax.sharding import PartitionSpec as P

D = 2048
HEAD_DIM = 128


epsilon_norm = 1e-06
rope_theta = 500000.0
masked_score = -1e30


def doc_positions(segment_row):
    length = segment_row.shape[0]
    indices = jnp.arange(length, dtype=jnp.int32)
    change = jnp.concatenate([jnp.ones((1,), jnp.bool_), segment_row[1:] != segment_row[:-1]])
    begins = lax.cummax(jnp.where(change, indices, 0), axis=0)
    return indices - begins


def rope_tables(positions):
    halfway = HEAD_DIM // 2
    inverse = rope_theta ** (-(jnp.arange(halfway, dtype=jnp.float32) * 2.0) / HEAD_DIM)
    angles = positions.astype(jnp.float32)[:, None] * inverse[None, :]
    return (jnp.cos(angles), jnp.sin(angles))


def rotate(field, cosine, sine_table):
    halfway = field.shape[-1] // 2
    first_half = field[..., :halfway]
    second = field[..., halfway:]
    cos_wide = cosine[:, None, :]
    sin_wide = sine_table[:, None, :]
    return jnp.concatenate(
        [first_half * cos_wide - second * sin_wide, second * cos_wide + first_half * sin_wide],
        axis=-1,
    )


def unrotate(field, cosine, sine_table):
    halfway = field.shape[-1] // 2
    first_half = field[..., :halfway]
    second = field[..., halfway:]
    cos_wide = cosine[:, None, :]
    sin_wide = sine_table[:, None, :]
    return jnp.concatenate(
        [first_half * cos_wide + second * sin_wide, second * cos_wide - first_half * sin_wide],
        axis=-1,
    )


def norm_back(upstream, normed, factor, gain):
    scaled = upstream * gain
    return factor * (scaled - normed * jnp.mean(scaled * normed, axis=1, keepdims=True))


def attention_scores(queries_r, keys_r, allowed):
    scores = jnp.einsum(
        "qhd,khd->hqk", queries_r, keys_r, preferred_element_type=jnp.float32
    ) * HEAD_DIM ** (-0.5)
    return jnp.where(allowed[None], scores, masked_score)


def product(left, right):
    return jnp.dot(left, right, preferred_element_type=jnp.float32)


def fetch_weights(shards):
    row_parts = (
        lax.all_gather(shards[0], "fsdp", axis=0, tiled=True),
        lax.all_gather(shards[1], "fsdp", axis=0, tiled=True),
        lax.all_gather(shards[2], "fsdp", axis=0, tiled=True),
        lax.all_gather(shards[3], "fsdp", axis=0, tiled=True),
        lax.all_gather(shards[4], "fsdp", axis=0, tiled=True),
        lax.all_gather(shards[5], "fsdp", axis=0, tiled=True),
        lax.all_gather(shards[6], "fsdp", axis=0, tiled=True),
        lax.all_gather(shards[7], "fsdp", axis=0, tiled=True),
        lax.all_gather(shards[8], "fsdp", axis=0, tiled=True),
    )
    col_parts = (
        lax.all_gather(shards[9], "fsdp", axis=1, tiled=True),
        lax.all_gather(shards[10], "fsdp", axis=1, tiled=True),
    )
    return tuple(row_parts) + tuple(col_parts)


def body(
    tokens,
    segment_ids,
    w_query,
    w_key,
    w_value,
    w_out,
    w_gate,
    w_up,
    w_down,
    gain_query,
    gain_key,
    gain_attn,
    gain_ffn,
    cotangent,
):
    shards = (
        w_query,
        w_key,
        w_value,
        w_gate,
        w_up,
        gain_query,
        gain_key,
        gain_attn,
        gain_ffn,
        w_out,
        w_down,
    )
    (
        query_full,
        key_full,
        value_full,
        gate_full,
        up_full,
        query_gain,
        key_gain,
        attn_gain,
        ffn_gain,
        out_full,
        down_full,
    ) = fetch_weights(shards)
    tensor_rank = lax.axis_index("tensor")
    local_width = query_full.shape[1]
    heads_here = local_width // HEAD_DIM
    start_col = tensor_rank * local_width
    gain_query_here = lax.dynamic_slice_in_dim(query_gain, start_col, local_width).astype(
        jnp.float32
    )
    gain_key_here = lax.dynamic_slice_in_dim(key_gain, start_col, local_width).astype(jnp.float32)
    attn_gain_f = attn_gain.astype(jnp.float32)
    ffn_gain_f = ffn_gain.astype(jnp.float32)
    gathered = lax.all_gather(tokens, "tensor", axis=0, tiled=True)
    length = gathered.shape[0]
    segment_row = segment_ids[0]
    queries = product(gathered, query_full)
    key_rows = product(gathered, key_full)
    values = product(gathered, value_full).astype(jnp.bfloat16)
    query_sq, key_sq = lax.psum(
        (jnp.sum(queries * queries, axis=1), jnp.sum(key_rows * key_rows, axis=1)), "tensor"
    )
    query_factor = lax.rsqrt(query_sq / D + epsilon_norm)[:, None]
    key_factor = lax.rsqrt(key_sq / D + epsilon_norm)[:, None]
    query_hat = queries * query_factor
    key_hat = key_rows * key_factor
    cosine, sine_table = rope_tables(doc_positions(segment_row))
    queries_r = rotate(
        (query_hat * gain_query_here).reshape(length, heads_here, HEAD_DIM), cosine, sine_table
    ).astype(jnp.bfloat16)
    keys_r = rotate(
        (key_hat * gain_key_here).reshape(length, heads_here, HEAD_DIM), cosine, sine_table
    ).astype(jnp.bfloat16)
    values_r = values.reshape(length, heads_here, HEAD_DIM)
    indices = jnp.arange(length)
    allowed = (segment_row[:, None] == segment_row[None, :]) & (
        indices[:, None] >= indices[None, :]
    )
    scores = attention_scores(queries_r, keys_r, allowed)
    top_score = jnp.max(scores, axis=-1, keepdims=True)
    log_total = top_score + jnp.log(jnp.sum(jnp.exp(scores - top_score), axis=-1, keepdims=True))
    attn_probs = jnp.exp(scores - log_total).astype(jnp.bfloat16)
    attended = (
        jnp.einsum("hqk,khd->qhd", attn_probs, values_r, preferred_element_type=jnp.float32)
        .astype(jnp.bfloat16)
        .reshape(length, local_width)
    )
    attn_rows = lax.psum_scatter(
        product(attended, out_full), "tensor", scatter_dimension=0, tiled=True
    )
    attn_factor = lax.rsqrt(jnp.mean(attn_rows * attn_rows, axis=1) + epsilon_norm)[:, None]
    attn_hat = attn_rows * attn_factor
    middle = tokens.astype(jnp.float32) + attn_hat * attn_gain_f
    middle_all = lax.all_gather(middle.astype(jnp.bfloat16), "tensor", axis=0, tiled=True)
    gate_pre = product(middle_all, gate_full)
    up_proj = product(middle_all, up_full)
    sigmoid_gate = jax.nn.sigmoid(gate_pre)
    silu_gate = gate_pre * sigmoid_gate
    hidden = (silu_gate * up_proj).astype(jnp.bfloat16)
    down_rows = lax.psum_scatter(
        product(hidden, down_full), "tensor", scatter_dimension=0, tiled=True
    )
    down_factor = lax.rsqrt(jnp.mean(down_rows * down_rows, axis=1) + epsilon_norm)[:, None]
    down_hat = down_rows * down_factor
    result = middle + down_hat * ffn_gain_f
    layer_out = result.astype(jnp.bfloat16)
    fenced = lax.optimization_barrier((result, shards))
    (
        query_full,
        key_full,
        value_full,
        gate_full,
        up_full,
        query_gain,
        key_gain,
        attn_gain,
        ffn_gain,
        out_full,
        down_full,
    ) = fetch_weights(fenced[1])
    grad_out = cotangent.astype(jnp.float32)
    ffn_gain_grad = jnp.sum(grad_out * down_hat, axis=0)
    grad_down = norm_back(grad_out, down_hat, down_factor, ffn_gain_f).astype(jnp.bfloat16)
    grad_down_all = lax.all_gather(grad_down, "tensor", axis=0, tiled=True)
    grad_hidden = product(grad_down_all, down_full.T)
    down_grad = product(hidden.T, grad_down_all)
    grad_gate = (
        grad_hidden * up_proj * sigmoid_gate * (1.0 + gate_pre * (1.0 - sigmoid_gate))
    ).astype(jnp.bfloat16)
    grad_up = (grad_hidden * silu_gate).astype(jnp.bfloat16)
    grad_middle_part = product(grad_gate, gate_full.T) + product(grad_up, up_full.T)
    gate_grad = product(middle_all.T, grad_gate)
    up_grad = product(middle_all.T, grad_up)
    grad_middle = grad_out + lax.psum_scatter(
        grad_middle_part, "tensor", scatter_dimension=0, tiled=True
    )
    attn_gain_grad = jnp.sum(grad_middle * attn_hat, axis=0)
    grad_attn = norm_back(grad_middle, attn_hat, attn_factor, attn_gain_f).astype(jnp.bfloat16)
    grad_attn_all = lax.all_gather(grad_attn, "tensor", axis=0, tiled=True)
    grad_attended = (
        product(grad_attn_all, out_full.T)
        .astype(jnp.bfloat16)
        .reshape(length, heads_here, HEAD_DIM)
    )
    out_grad = product(attended.T, grad_attn_all)
    probs_again = jnp.exp(attention_scores(queries_r, keys_r, allowed) - log_total)
    grad_values = jnp.einsum(
        "hqk,qhd->khd",
        probs_again.astype(jnp.bfloat16),
        grad_attended,
        preferred_element_type=jnp.float32,
    ).astype(jnp.bfloat16)
    grad_probs = jnp.einsum(
        "qhd,khd->hqk", grad_attended, values_r, preferred_element_type=jnp.float32
    )
    grad_scores = (
        probs_again * (grad_probs - jnp.sum(probs_again * grad_probs, axis=-1, keepdims=True))
    ).astype(jnp.bfloat16)
    score_scale = HEAD_DIM ** (-0.5)
    grad_queries_r = (
        jnp.einsum("hqk,khd->qhd", grad_scores, keys_r, preferred_element_type=jnp.float32)
        * score_scale
    )
    grad_keys_r = (
        jnp.einsum("hqk,qhd->khd", grad_scores, queries_r, preferred_element_type=jnp.float32)
        * score_scale
    )
    grad_query_n = unrotate(grad_queries_r, cosine, sine_table).reshape(length, local_width)
    grad_key_n = unrotate(grad_keys_r, cosine, sine_table).reshape(length, local_width)
    zeros_full = jnp.zeros((D,), jnp.float32)
    query_gain_part = lax.dynamic_update_slice_in_dim(
        zeros_full, jnp.sum(grad_query_n * query_hat, axis=0), start_col, 0
    )
    key_gain_part = lax.dynamic_update_slice_in_dim(
        zeros_full, jnp.sum(grad_key_n * key_hat, axis=0), start_col, 0
    )
    query_scaled = grad_query_n * gain_query_here
    key_scaled = grad_key_n * gain_key_here
    query_dot, key_dot, query_gain_grad, key_gain_grad, attn_gain_sum, ffn_gain_sum = (
        lax.psum(jnp.sum(query_scaled * query_hat, axis=1).astype(jnp.bfloat16), "tensor").astype(
            jnp.float32
        ),
        lax.psum(jnp.sum(key_scaled * key_hat, axis=1).astype(jnp.bfloat16), "tensor").astype(
            jnp.float32
        ),
        lax.psum(query_gain_part.astype(jnp.bfloat16), "tensor").astype(jnp.float32),
        lax.psum(key_gain_part.astype(jnp.bfloat16), "tensor").astype(jnp.float32),
        lax.psum(attn_gain_grad.astype(jnp.bfloat16), "tensor").astype(jnp.float32),
        lax.psum(ffn_gain_grad.astype(jnp.bfloat16), "tensor").astype(jnp.float32),
    )
    grad_queries = (query_factor * (query_scaled - query_hat * (query_dot / D)[:, None])).astype(
        jnp.bfloat16
    )
    grad_keys = (key_factor * (key_scaled - key_hat * (key_dot / D)[:, None])).astype(jnp.bfloat16)
    grad_values_flat = grad_values.reshape(length, local_width)
    grad_tokens_part = (
        product(grad_queries, query_full.T)
        + product(grad_keys, key_full.T)
        + product(grad_values_flat, value_full.T)
    )
    grad_input = grad_middle + lax.psum_scatter(
        grad_tokens_part.astype(jnp.bfloat16), "tensor", scatter_dimension=0, tiled=True
    ).astype(jnp.float32)
    query_grad = product(gathered.T, grad_queries)
    key_grad = product(gathered.T, grad_keys)
    value_grad = product(gathered.T, grad_values_flat)
    row_grads = (
        lax.psum_scatter(query_grad, "fsdp", scatter_dimension=0, tiled=True),
        lax.psum_scatter(key_grad, "fsdp", scatter_dimension=0, tiled=True),
        lax.psum_scatter(value_grad, "fsdp", scatter_dimension=0, tiled=True),
        lax.psum_scatter(gate_grad, "fsdp", scatter_dimension=0, tiled=True),
        lax.psum_scatter(up_grad, "fsdp", scatter_dimension=0, tiled=True),
        lax.psum_scatter(query_gain_grad, "fsdp", scatter_dimension=0, tiled=True),
        lax.psum_scatter(key_gain_grad, "fsdp", scatter_dimension=0, tiled=True),
        lax.psum_scatter(attn_gain_sum, "fsdp", scatter_dimension=0, tiled=True),
        lax.psum_scatter(ffn_gain_sum, "fsdp", scatter_dimension=0, tiled=True),
    )
    col_grads = (
        lax.psum_scatter(out_grad, "fsdp", scatter_dimension=1, tiled=True),
        lax.psum_scatter(down_grad, "fsdp", scatter_dimension=1, tiled=True),
    )
    return (
        layer_out,
        grad_input,
        row_grads[0],
        row_grads[1],
        row_grads[2],
        col_grads[0],
        row_grads[3],
        row_grads[4],
        col_grads[1],
        row_grads[5],
        row_grads[6],
        row_grads[7],
        row_grads[8],
    )


def solution(mesh):
    placed = (
        P(("fsdp", "tensor"), None),
        P("fsdp", None),
        P("fsdp", "tensor"),
        P("fsdp", "tensor"),
        P("fsdp", "tensor"),
        P("tensor", "fsdp"),
        P("fsdp", "tensor"),
        P("fsdp", "tensor"),
        P("tensor", "fsdp"),
        P("fsdp"),
        P("fsdp"),
        P("fsdp"),
        P("fsdp"),
        P(("fsdp", "tensor"), None),
    )
    return jax.shard_map(
        body,
        mesh=mesh,
        in_specs=placed,
        out_specs=(
            P(("fsdp", "tensor"), None),
            P(("fsdp", "tensor"), None),
            P("fsdp", "tensor"),
            P("fsdp", "tensor"),
            P("fsdp", "tensor"),
            P("tensor", "fsdp"),
            P("fsdp", "tensor"),
            P("fsdp", "tensor"),
            P("tensor", "fsdp"),
            P("fsdp"),
            P("fsdp"),
            P("fsdp"),
            P("fsdp"),
        ),
        check_vma=False,
    )
```

profile of v0, /device:TPU:0, one launch (start us, length us, event | category | flops | bytes accessed | tf_op | source)
XLA Modules:
  0.0 2965.8 jit_solution(9770110612626096877)
XLA Ops:
  11.3 23.0 all-gather
  53.4 39.2 %all-gather.27.cloned.1.call-done = bf16[2048,1024]{1,0:T(8,128)(2,1)} async-done(((bf16[128,1024]{1,0:T(8,128)(2,1)}), bf16[2048,1024]{1,0:T(8,128)(2,1)}) %all-gather.27.cloned.1.call-update) | async-done | bytes 4194320 | tf_op jit(solution)/shard_map/all_gather | solution.py:72
  97.1 46.7 %all-gather.29.cloned.1.call-done = bf16[2048,1024]{1,0:T(8,128)(2,1)} async-done(((bf16[128,1024]{1,0:T(8,128)(2,1)}), bf16[2048,1024]{1,0:T(8,128)(2,1)}) %all-gather.29.cloned.1.call-update) | async-done | bytes 4194320 | tf_op jit(solution)/shard_map/all_gather | solution.py:73
  161.6 33.4 %all-gather.25.cloned.1.call-done = bf16[2048,1024]{1,0:T(8,128)(2,1)} async-done(((bf16[128,1024]{1,0:T(8,128)(2,1)}), bf16[2048,1024]{1,0:T(8,128)(2,1)}) %all-gather.25.cloned.1.call-update) | async-done | bytes 4194320 | tf_op jit(solution)/shard_map/all_gather | solution.py:74
  200.7 48.0 %all-gather.31.cloned.1.call-done = bf16[1024,2048]{1,0:T(8,128)(2,1)} async-done(((bf16[1024,128]{1,0:T(8,128)(2,1)}), bf16[1024,2048]{1,0:T(8,128)(2,1)}) %all-gather.31.cloned.1.call-update) | async-done | bytes 4194320 | tf_op jit(solution)/shard_map/all_gather | solution.py:83
  255.0 18.5 all-gather.2
  273.6 22.5 reduce-scatter.12.cloned.1.call-done
  301.5 25.0 all-gather.33.cloned.1.call-done
  326.6 129.3 %all-gather.35.cloned.1.call-done = bf16[2048,4096]{1,0:T(8,128)(2,1)} async-done(((bf16[128,4096]{1,0:T(8,128)(2,1)}), bf16[2048,4096]{1,0:T(8,128)(2,1)}) %all-gather.35.cloned.1.call-update) | async-done | bytes 16777232 | tf_op jit(solution)/shard_map/all_gather | solution.py:75
  468.2 115.1 %all-gather.37.cloned.1.call-done = bf16[2048,4096]{1,0:T(8,128)(2,1)} async-done(((bf16[128,4096]{1,0:T(8,128)(2,1)}), bf16[2048,4096]{1,0:T(8,128)(2,1)}) %all-gather.37.cloned.1.call-update) | async-done | bytes 16777232 | tf_op jit(solution)/shard_map/all_gather | solution.py:76
  599.6 114.5 %all-gather.39.cloned.1.call-done = bf16[4096,2048]{1,0:T(8,128)(2,1)} async-done(((bf16[4096,128]{1,0:T(8,128)(2,1)}), bf16[4096,2048]{1,0:T(8,128)(2,1)}) %all-gather.39.cloned.1.call-update) | async-done | bytes 16777232 | tf_op jit(solution)/shard_map/all_gather | solution.py:84
  727.1 19.1 all-gather.3
  746.3 21.9 reduce-scatter.14.cloned.1.call-done
  777.3 23.2 all-gather.41.cloned.1.call-done
  800.5 132.5 %all-gather.43.cloned.1.call-done = bf16[4096,2048]{1,0:T(8,128)(2,1)} async-done(((bf16[4096,128]{1,0:T(8,128)(2,1)}), bf16[4096,2048]{1,0:T(8,128)(2,1)}) %all-gather.43.cloned.1.call-update) | async-done | bytes 16777232 | tf_op jit(solution)/shard_map/all_gather | solution.py:84
  949.8 110.4 %all-gather.45.cloned.1.call-done = bf16[2048,4096]{1,0:T(8,128)(2,1)} async-done(((bf16[128,4096]{1,0:T(8,128)(2,1)}), bf16[2048,4096]{1,0:T(8,128)(2,1)}) %all-gather.45.cloned.1.call-update) | async-done | bytes 16777232 | tf_op jit(solution)/shard_map/all_gather | solution.py:75
  1072.6 114.7 %all-gather.47.cloned.1.call-done = bf16[2048,4096]{1,0:T(8,128)(2,1)} async-done(((bf16[128,4096]{1,0:T(8,128)(2,1)}), bf16[2048,4096]{1,0:T(8,128)(2,1)}) %all-gather.47.cloned.1.call-update) | async-done | bytes 16777232 | tf_op jit(solution)/shard_map/all_gather | solution.py:76
  1201.0 41.0 %reduce-scatter.16.cloned.1.call-done = f32[192,2048]{1,0:T(8,128)} async-done(((f32[384,2048]{1,0:T(8,128)}), f32[192,2048]{1,0:T(8,128)}) %reduce-scatter.16.cloned.1.call-update) | async-done | bytes 1572880 | tf_op jit(solution)/shard_map/reduce_scatter | solution.py:221
  1247.8 49.7 %all-gather.51.cloned.1.call-done = bf16[1024,2048]{1,0:T(8,128)(2,1)} async-done(((bf16[1024,128]{1,0:T(8,128)(2,1)}), bf16[1024,2048]{1,0:T(8,128)(2,1)}) %all-gather.51.cloned.1.call-update) | async-done | bytes 4194320 | tf_op jit(solution)/shard_map/all_gather | solution.py:83
  1297.5 27.5 all-gather.49.cloned.1.call-done
  1384.0 45.4 %all-gather.55.cloned.1.call-done = bf16[2048,1024]{1,0:T(8,128)(2,1)} async-done(((bf16[128,1024]{1,0:T(8,128)(2,1)}), bf16[2048,1024]{1,0:T(8,128)(2,1)}) %all-gather.55.cloned.1.call-update) | async-done | bytes 4194320 | tf_op jit(solution)/shard_map/all_gather | solution.py:73
  1435.1 45.8 %all-gather.57.cloned.1.call-done = bf16[2048,1024]{1,0:T(8,128)(2,1)} async-done(((bf16[128,1024]{1,0:T(8,128)(2,1)}), bf16[2048,1024]{1,0:T(8,128)(2,1)}) %all-gather.57.cloned.1.call-update) | async-done | bytes 4194320 | tf_op jit(solution)/shard_map/all_gather | solution.py:74
  1510.3 18.9 fusion.37
  1539.6 17.9 fusion.35
  1557.5 17.5 fusion.36
  1577.0 60.5 %all-reduce.4 = (f32[2048]{0:T(1024)S(1)}, f32[2048]{0:T(1024)S(1)}, f32[2048]{0:T(1024)S(1)}, f32[2048]{0:T(1024)S(1)}) all-reduce(bf16[2048]{0:T(1024)(128)(2,1)S(1)} %get-tuple-element.80, bf16[2048]{0:T(1024)(128)(2,1)S(1)} %get-tuple-element.81, ...), channel_id=13, replica_groups=mesh['fsdp'=16,'tensor'=2] {'fsdp'}, use_global_device_ids=true, to_apply=%region_30.31.clone | all-reduce | flops 8192 | bytes 49152
  1644.5 86.5 %reduce-scatter.22.cloned.1.call-done = f32[128,1024]{0,1:T(8,128)} async-done(((f32[2048,1024]{0,1:T(8,128)}), f32[128,1024]{0,1:T(8,128)}) %reduce-scatter.22.cloned.1.call-update) | async-done | bytes 524304 | tf_op jit(solution)/shard_map/reduce_scatter | solution.py:296
  1733.1 106.7 %reduce-scatter.24.cloned.1.call-done = f32[128,1024]{0,1:T(8,128)} async-done(((f32[2048,1024]{0,1:T(8,128)}), f32[128,1024]{0,1:T(8,128)}) %reduce-scatter.24.cloned.1.call-update) | async-done | bytes 524304 | tf_op jit(solution)/shard_map/reduce_scatter | solution.py:297
  1841.8 335.0 %reduce-scatter.32.cloned.1.call-done = f32[4096,128]{1,0:T(8,128)} async-done(((f32[4096,2048]{1,0:T(8,128)}), f32[4096,128]{1,0:T(8,128)}) %reduce-scatter.32.cloned.1.call-update) | async-done | bytes 2097168 | tf_op jit(solution)/shard_map/reduce_scatter | solution.py:307
  2176.8 108.4 %reduce-scatter.26.cloned.1.call-done = f32[1024,128]{1,0:T(8,128)} async-done(((f32[1024,2048]{1,0:T(8,128)}), f32[1024,128]{1,0:T(8,128)}) %reduce-scatter.26.cloned.1.call-update) | async-done | bytes 524304 | tf_op jit(solution)/shard_map/reduce_scatter | solution.py:306
  2285.2 337.2 %reduce-scatter.28.cloned.1.call-done = f32[128,4096]{1,0:T(8,128)} async-done(((f32[2048,4096]{1,0:T(8,128)}), f32[128,4096]{1,0:T(8,128)}) %reduce-scatter.28.cloned.1.call-update) | async-done | bytes 2097168 | tf_op jit(solution)/shard_map/reduce_scatter | solution.py:298
  2622.4 336.6 %reduce-scatter.30.cloned.1.call-done = f32[128,4096]{1,0:T(8,128)} async-done(((f32[2048,4096]{1,0:T(8,128)}), f32[128,4096]{1,0:T(8,128)}) %reduce-scatter.30.cloned.1.call-update) | async-done | bytes 2097168 | tf_op jit(solution)/shard_map/reduce_scatter | solution.py:299
  (268 shorter events, 278.2 us)
Async XLA Ops:
  7.2 46.2 %all-gather.23.cloned.1.call-start = ((), (), s32[]{:S(2)}) async-start(), calls=%async_computation.11 | async-start | bytes 2359296 | tf_op jit(solution)/shard_map/all_gather | solution.py:141
  7.9 84.7 %all-gather.27.cloned.1.call-start = ((), (), s32[]{:S(2)}) async-start(), calls=%async_computation.13 | async-start | bytes 4456448 | tf_op jit(solution)/shard_map/all_gather | solution.py:72
  8.7 135.2 %all-gather.29.cloned.1.call-start = ((), (), s32[]{:S(2)}) async-start(), calls=%async_computation.14 | async-start | bytes 4456448 | tf_op jit(solution)/shard_map/all_gather | solution.py:73
  9.4 185.5 %all-gather.25.cloned.1.call-start = ((), (), s32[]{:S(2)}) async-start(), calls=%async_computation.12 | async-start | bytes 4456448 | tf_op jit(solution)/shard_map/all_gather | solution.py:74
  10.0 238.7 %all-gather.31.cloned.1.call-start = ((), (), s32[]{:S(2)}) async-start(), calls=%async_computation.15 | async-start | bytes 4456448 | tf_op jit(solution)/shard_map/all_gather | solution.py:83
  10.6 285.5 %reduce-scatter.12.cloned.1.call-start = ((), (), s32[]{:S(2)}) async-start(), calls=%async_computation.16 | async-start | bytes 4718592 | tf_op jit(solution)/shard_map/reduce_scatter | solution.py:175
  51.7 101.8 %copy-start.42 = (f32[1024]{0:T(1024)}, f32[1024]{0:T(1024)S(1)}, u32[]{:S(2)}) copy-start(f32[1024]{0:T(1024)S(1)} %dynamic-slice_convert_fusion.1) | copy-start | bytes 12292
  51.8 102.7 %copy-start.40 = (f32[1024]{0:T(1024)}, f32[1024]{0:T(1024)S(1)}, u32[]{:S(2)}) copy-start(f32[1024]{0:T(1024)S(1)} %dynamic-slice_convert_fusion) | copy-start | bytes 12292
  254.4 72.1 %all-gather.33.cloned.1.call-start = ((), (), s32[]{:S(2)}) async-start(), calls=%async_computation.17 | async-start | bytes 2359296 | tf_op jit(solution)/shard_map/all_gather | solution.py:181
  299.2 156.7 %all-gather.35.cloned.1.call-start = ((), (), s32[]{:S(2)}) async-start(), calls=%async_computation.18 | async-start | bytes 17825792 | tf_op jit(solution)/shard_map/all_gather | solution.py:75
  299.9 283.4 %all-gather.37.cloned.1.call-start = ((), (), s32[]{:S(2)}) async-start(), calls=%async_computation.19 | async-start | bytes 17825792 | tf_op jit(solution)/shard_map/all_gather | solution.py:76
  300.7 413.5 %all-gather.39.cloned.1.call-start = ((), (), s32[]{:S(2)}) async-start(), calls=%async_computation.20 | async-start | bytes 17825792 | tf_op jit(solution)/shard_map/all_gather | solution.py:84
  301.3 466.9 %reduce-scatter.14.cloned.1.call-start = ((), (), s32[]{:S(2)}) async-start(), calls=%async_computation.21 | async-start | bytes 4718592 | tf_op jit(solution)/shard_map/reduce_scatter | solution.py:187
  326.6 256.8 %copy-start.18 = (bf16[384,2048]{1,0:T(8,128)(2,1)S(1)}, bf16[384,2048]{1,0:T(8,128)(2,1)}, u32[]{:S(2)}) copy-start(bf16[384,2048]{1,0:T(8,128)(2,1)} %all-gather.33.cloned.1.call-done) | copy-start | bytes 4718596
  726.5 74.0 %all-gather.41.cloned.1.call-start = ((), (), s32[]{:S(2)}) async-start(), calls=%async_computation.22 | async-start | bytes 2359296 | tf_op jit(solution)/shard_map/all_gather | solution.py:211
  773.2 159.9 %all-gather.43.cloned.1.call-start = ((), (), s32[]{:S(2)}) async-start(), calls=%async_computation.23 | async-start | bytes 17825792 | tf_op jit(solution)/shard_map/all_gather | solution.py:84
  775.7 284.5 %all-gather.45.cloned.1.call-start = ((), (), s32[]{:S(2)}) async-start(), calls=%async_computation.24 | async-start | bytes 17825792 | tf_op jit(solution)/shard_map/all_gather | solution.py:75
  776.3 411.0 %all-gather.47.cloned.1.call-start = ((), (), s32[]{:S(2)}) async-start(), calls=%async_computation.25 | async-start | bytes 17825792 | tf_op jit(solution)/shard_map/all_gather | solution.py:76
  776.9 465.1 %reduce-scatter.16.cloned.1.call-start = ((), (), s32[]{:S(2)}) async-start(), calls=%async_computation.26 | async-start | bytes 4718592 | tf_op jit(solution)/shard_map/reduce_scatter | solution.py:221
  1200.3 97.2 %all-gather.51.cloned.1.call-start = ((), (), s32[]{:S(2)}) async-start(), calls=%async_computation.28 | async-start | bytes 4456448 | tf_op jit(solution)/shard_map/all_gather | solution.py:83
  1200.9 124.0 %all-gather.49.cloned.1.call-start = ((), (), s32[]{:S(2)}) async-start(), calls=%async_computation.27 | async-start | bytes 2359296 | tf_op jit(solution)/shard_map/all_gather | solution.py:226
  1245.5 132.6 %all-gather.53.cloned.1.call-start = ((), (), s32[]{:S(2)}) async-start(), calls=%async_computation.29 | async-start | bytes 4456448 | tf_op jit(solution)/shard_map/all_gather | solution.py:72
  1246.3 183.2 %all-gather.55.cloned.1.call-start = ((), (), s32[]{:S(2)}) async-start(), calls=%async_computation.30 | async-start | bytes 4456448 | tf_op jit(solution)/shard_map/all_gather | solution.py:73
  1246.9 234.1 %all-gather.57.cloned.1.call-start = ((), (), s32[]{:S(2)}) async-start(), calls=%async_computation.31 | async-start | bytes 4456448 | tf_op jit(solution)/shard_map/all_gather | solution.py:74
  1247.6 392.3 %reduce-scatter.18.cloned.1.call-start = ((), (), s32[]{:S(2)}) async-start(), calls=%async_computation.32 | async-start | bytes 2359296 | tf_op jit(solution)/shard_map/reduce_scatter | solution.py:288
  1488.3 154.2 %reduce-scatter.20.cloned.1.call-start = ((), (), s32[]{:S(2)}) async-start(), calls=%async_computation.33 | async-start | bytes 8912896 | tf_op jit(solution)/shard_map/reduce_scatter | solution.py:295
  1495.4 235.7 %reduce-scatter.22.cloned.1.call-start = ((), (), s32[]{:S(2)}) async-start(), calls=%async_computation.34 | async-start | bytes 8912896 | tf_op jit(solution)/shard_map/reduce_scatter | solution.py:296
  1502.2 337.6 %reduce-scatter.24.cloned.1.call-start = ((), (), s32[]{:S(2)}) async-start(), calls=%async_computation.35 | async-start | bytes 8912896 | tf_op jit(solution)/shard_map/reduce_scatter | solution.py:297
  1508.9 667.9 %reduce-scatter.32.cloned.1.call-start = ((), (), s32[]{:S(2)}) async-start(), calls=%async_computation.39 | async-start | bytes 35651584 | tf_op jit(solution)/shard_map/reduce_scatter | solution.py:307
  1529.2 756.0 %reduce-scatter.26.cloned.1.call-start = ((), (), s32[]{:S(2)}) async-start(), calls=%async_computation.36 | async-start | bytes 8912896 | tf_op jit(solution)/shard_map/reduce_scatter | solution.py:306
  1538.1 1084.4 %reduce-scatter.28.cloned.1.call-start = ((), (), s32[]{:S(2)}) async-start(), calls=%async_computation.37 | async-start | bytes 35651584 | tf_op jit(solution)/shard_map/reduce_scatter | solution.py:298
  1557.5 1401.6 %reduce-scatter.30.cloned.1.call-start = ((), (), s32[]{:S(2)}) async-start(), calls=%async_computation.38 | async-start | bytes 35651584 | tf_op jit(solution)/shard_map/reduce_scatter | solution.py:299
  (55 other events, 512.5 us)
Sparse Core Ops, SparseCore 0:
  9.6 29.8 all-gather.22
  41.7 50.8 all-gather.26
  94.8 49.0 all-gather.28
  145.9 49.0 all-gather.24
  197.0 51.7 all-gather.30
  254.5 41.5 reduce-scatter.11
  299.3 27.2 all-gather.32
  328.9 126.8 all-gather.34
  458.3 125.0 all-gather.36
  585.6 128.5 all-gather.38
  726.6 41.5 reduce-scatter.13
  773.3 27.2 all-gather.40
  802.7 130.3 all-gather.42
  935.1 125.0 all-gather.44
  1062.2 125.0 all-gather.46
  1200.5 41.5 reduce-scatter.15
  1244.2 53.1 all-gather.50
  1299.5 25.3 all-gather.48
  1327.3 50.7 all-gather.52
  1380.3 49.0 all-gather.54
  1431.8 49.0 all-gather.56
  1488.4 24.5 reduce-scatter.17
  1517.1 105.3 reduce-scatter.19
  1626.4 104.5 reduce-scatter.21
  1735.1 104.5 reduce-scatter.23
  1844.4 332.3 reduce-scatter.31
  2181.3 103.8 reduce-scatter.25
  2290.1 332.3 reduce-scatter.27
  2627.3 331.7 reduce-scatter.29
where the time goes:
time: 2970 us
  waiting for transfers between devices  2520 us (85%)
  matrix products  216 us (7%)
  blocking collectives  151 us (5%)
  other arithmetic  32.8 us (1%)
    reduce_scatter x1, waiting for transfers between devices, body(): lax.psum_scatter(gate_grad, 'fsdp', scatter_dimension=0, tiled=True)  337 us
    reduce_scatter x1, waiting for transfers between devices, body(): lax.psum_scatter(up_grad, 'fsdp', scatter_dimension=0, tiled=True)  337 us
    reduce_scatter x1, waiting for transfers between devices, body(): lax.psum_scatter(down_grad, 'fsdp', scatter_dimension=1, tiled=True)  335 us
    all_gather x2, waiting for transfers between devices, fetch_weights(): lax.all_gather(shards[10], 'fsdp', axis=1, tiled=True)  247 us
    all_gather x2, waiting for transfers between devices, fetch_weights(): lax.all_gather(shards[3], 'fsdp', axis=0, tiled=True)  240 us
    all_gather x2, waiting for transfers between devices, fetch_weights(): lax.all_gather(shards[4], 'fsdp', axis=0, tiled=True)  230 us
    dot_general x21, matrix products, product(): return jnp.dot(left, right, preferred_element_type=jnp.float32)  204 us
    reduce_scatter x1, waiting for transfers between devices, body(): lax.psum_scatter(out_grad, 'fsdp', scatter_dimension=1, tiled=True)  108 us
  transfers between devices with their start and end apart: 29, of which 26 were waited for; matrix products, arithmetic and copies ran while one was open for 7% of the time, Pallas kernels for 0%

commit v1 on v0

v1 whole, which is shorter than its diff:
```python
import functools

import jax
import jax.numpy as jnp
from jax import lax
from jax.experimental import pallas as pl
from jax.experimental.pallas import tpu as pltpu
from jax.sharding import PartitionSpec as P

HEAD_DIM = 128
epsilon_norm = 1e-06
rope_theta = 500000.0
masked_score = -1e30
MESH = pl.DeviceIdType.MESH
SWAP = [(0, 1), (1, 0)]


def ring_chip(pos, n):
    if n != 8:
        return pos
    x = pos // 4
    z = pos + x * (7 - 2 * pos)
    return z * 2 + x


def ring_pos(chip, n):
    if n != 8:
        return chip
    x = chip % 2
    z = chip // 2
    return z + x * (7 - 2 * z)


class Ring:
    def __init__(self, n):
        self.n = n
        self.h = n // 2
        self.f = lax.axis_index("fsdp")
        self.t = lax.axis_index("tensor")
        self.c = self.f % 2
        self.pos = ring_pos(self.f // 2, n)
        self.next = (self.chip(1) * 2 + self.c, self.t)
        self.prev = (self.chip(-1) * 2 + self.c, self.t)
        self.mate = (self.f + 1 - 2 * self.c, self.t)

    def chip(self, offset):
        return ring_chip((self.pos + offset + self.n) % self.n, self.n)

    def greet(self):
        barrier = pltpu.get_barrier_semaphore()
        for peer in (self.next, self.prev, self.mate):
            pl.semaphore_signal(barrier, inc=1, device_id=peer, device_id_type=MESH)
        pl.semaphore_wait(barrier, 3)


def remote(src, dst, send, recv, peer):
    return pltpu.make_async_remote_copy(
        src_ref=src,
        dst_ref=dst,
        send_sem=send,
        recv_sem=recv,
        device_id=peer,
        device_id_type=MESH,
    )


def gather_kernel(n, w_ref, g_ref, ssem, rsem, msend, mrecv, osend, orecv, lsem):
    ring = Ring(n)
    h = ring.h
    count, rows, _ = w_ref.shape
    half = rows // 2
    ring.greet()

    def slot(w, offset):
        return (ring.chip(offset) * 2 + ring.c, w)

    def part(ref, piece):
        if piece is None:
            return ref
        return ref.at[pl.ds(piece * half, half), :]

    def hop(w, way, d, piece):
        origin = -d if way == 0 else d
        s, _ = slot(w, origin)
        src = w_ref.at[w] if isinstance(d, int) and d == 0 else g_ref.at[w, s]
        return remote(
            part(src, piece),
            part(g_ref.at[w, s], piece),
            ssem.at[w, way, d % 4],
            rsem.at[w, way, d % 4],
            ring.next if way == 0 else ring.prev,
        )

    def share(w, way, d, piece):
        origin = -1 - d if way == 0 else 1 + d
        s, _ = slot(w, origin)
        ref = part(g_ref.at[w, s], piece)
        return remote(ref, ref, msend.at[w, way, d % 4], mrecv.at[w, way, d % 4], ring.mate)

    def share_in(w, way, d, piece):
        origin = -1 - d if way == 0 else 1 + d
        s = ring.chip(origin) * 2 + 1 - ring.c
        ref = part(g_ref.at[w, s], piece)
        return remote(ref, ref, msend.at[w, way, d % 4], mrecv.at[w, way, d % 4], ring.mate)

    def arrival(w, way, d, piece):
        origin = -1 - d if way == 0 else 1 + d
        s, _ = slot(w, origin)
        ref = part(g_ref.at[w, s], piece)
        return remote(
            ref,
            ref,
            ssem.at[w, way, d % 4],
            rsem.at[w, way, d % 4],
            ring.next if way == 0 else ring.prev,
        )

    def own(w):
        return (
            remote(w_ref.at[w], g_ref.at[w, ring.f], osend.at[w], orecv.at[w], ring.mate),
            pltpu.make_async_copy(w_ref.at[w], g_ref.at[w, ring.f], lsem.at[w]),
        )

    def begin(w):
        for way in (0, 1):
            hop(w, way, 0, None).start()
        for copy in own(w):
            copy.start()

    def piece_of(d, way):
        return way if d == h - 1 else None

    begin(0)
    for w in range(count):
        if w + 1 < count:
            begin(w + 1)

        def step(d, carry):
            for way in (0, 1):
                arrival(w, way, d, None).wait_recv()
                hop(w, way, d + 1, None).start()
                share(w, way, d, None).start()
            return carry

        if h - 2 <= 4:
            for d in range(h - 2):
                step(d, 0)
        else:
            lax.fori_loop(0, h - 2, step, 0)
        for d in (h - 2, h - 1):
            for way in (0, 1):
                arrival(w, way, d, piece_of(d, way)).wait_recv()
                if d == h - 2:
                    hop(w, way, h - 1, way).start()
                share(w, way, d, piece_of(d, way)).start()

        def finish(d, carry):
            for way in (0, 1):
                hop(w, way, d, None).wait_send()
                share(w, way, d, None).wait_send()
                share_in(w, way, d, None).wait_recv()
            return carry

        if h - 1 <= 4:
            for d in range(h - 1):
                finish(d, 0)
        else:
            lax.fori_loop(0, h - 1, finish, 0)
        for way in (0, 1):
            hop(w, way, h - 1, way).wait_send()
            share(w, way, h - 1, way).wait_send()
            share_in(w, way, h - 1, way).wait_recv()
        first, second = own(w)
        first.wait_send()
        remote(
            g_ref.at[w, ring.mate[0]],
            g_ref.at[w, ring.mate[0]],
            osend.at[w],
            orecv.at[w],
            ring.mate,
        ).wait_recv()
        second.wait()


def gather_weights(shards, n):
    count, rows, width = shards.shape
    dma = pltpu.SemaphoreType.DMA
    return pl.pallas_call(
        functools.partial(gather_kernel, n),
        out_shape=jax.ShapeDtypeStruct((count, 2 * n, rows, width), shards.dtype),
        in_specs=[pl.BlockSpec(memory_space=pl.ANY)],
        out_specs=pl.BlockSpec(memory_space=pl.ANY),
        scratch_shapes=[
            dma((count, 2, 4)),
            dma((count, 2, 4)),
            dma((count, 2, 4)),
            dma((count, 2, 4)),
            dma((count,)),
            dma((count,)),
            dma((count,)),
        ],
        compiler_params=pltpu.CompilerParams(collective_id=0, has_side_effects=True),
        name="gather_weights",
    )(shards)


def scatter_kernel(
    n,
    left_hbm,
    right_hbm,
    out_hbm,
    left,
    right,
    partial,
    mate_out,
    mate_in,
    ring_in,
    ring_out,
    stage,
    lsem,
    rsem,
    msend,
    mrecv,
    ssem,
    isem,
    osem,
):
    ring = Ring(n)
    h = ring.h
    count = right.shape[0]
    rows = mate_out.shape[1]
    half = rows // 2
    wide = mate_out.shape[2]
    tile = 512
    tiles = wide // tile
    load_left = [pltpu.make_async_copy(left_hbm.at[i], left.at[i], lsem.at[i]) for i in range(4)]
    load_right = [pltpu.make_async_copy(right_hbm.at[i], right.at[i], rsem.at[i]) for i in range(4)]
    for i in range(4):
        load_left[i].start()
        load_right[i].start()
    ring.greet()
    for i in range(4):
        load_left[i].wait()
        load_right[i].wait()

    def mate_copy(pslot, slot):
        return remote(
            mate_out.at[pslot], mate_in.at[slot], msend.at[pslot], mrecv.at[slot], ring.mate
        )

    def prepare(w, dest, sub, pslot, slot):
        base = pl.multiple_of(ring.chip(dest) * (2 * rows), 2 * rows)

        def one(i, carry):
            col = pl.multiple_of(i * tile, tile)
            source = pl.multiple_of(sub * wide + i * tile, tile)
            which = w - w // 2 + (w // 3) * ((sub * tiles + i) // (3 * tiles // 2))
            partial[pslot, :, pl.ds(col, tile)] = jnp.dot(
                left[which, pl.ds(base, 2 * rows), :],
                right[w, :, pl.ds(source, tile)],
                preferred_element_type=jnp.float32,
            )
            mate_out[pslot, :, pl.ds(col, tile)] = partial[
                pslot, pl.ds(pl.multiple_of((1 - ring.c) * rows, rows), rows), pl.ds(col, tile)
            ].astype(jnp.bfloat16)
            return carry

        lax.fori_loop(0, tiles, one, 0)
        mate_copy(pslot, slot).start()

    def ring_copy(way, s, sub, span):
        view = pl.ds(0, rows) if span is None else pl.ds(span * half, half)
        return remote(
            ring_out.at[way, sub, view, :],
            ring_in.at[way, s % 4, sub, view, :],
            ssem.at[way, sub],
            isem.at[way, s % 4, sub],
            ring.next if way == 0 else ring.prev,
        )

    def mine(pslot, slot, col, lo, size):
        start = pl.multiple_of(ring.c * rows + lo, half)
        return partial[pslot, pl.ds(start, size), pl.ds(col, tile)] + mate_in[
            slot, pl.ds(lo, size), pl.ds(col, tile)
        ].astype(jnp.float32)

    def over_tiles(fn):
        def one(i, carry):
            fn(pl.multiple_of(i * tile, tile))
            return carry

        lax.fori_loop(0, tiles, one, 0)

    def arrived(pslot, slot):
        mate_copy(pslot, slot).wait_recv()

    def group(entries, w):
        def lead(k):
            dest, sub, slot, _ = entries[k]
            if k >= 2:
                mate_copy(k % 2, slot).wait_send()
            prepare(w, dest, sub, k % 2, slot)

        lead(0)
        for k, (dest, sub, slot, act) in enumerate(entries):
            if k + 1 < len(entries):
                lead(k + 1)
            arrived(k % 2, slot)
            act(k % 2, slot)
        for k in range(len(entries))[-2:]:
            mate_copy(k % 2, entries[k][2]).wait_send()

    def weight(w, carry):
        def first(sub):
            def act(pslot, slot):
                @pl.when(w > 0)
                def _():
                    for way in (0, 1):
                        ring_copy(way, h - 1, sub, None).wait_send()

                def fill(col):
                    for way in (0, 1):
                        lo = way * half
                        ring_out[way, sub, pl.ds(lo, half), pl.ds(col, tile)] = mine(
                            pslot, slot, col, lo, half
                        ).astype(jnp.bfloat16)

                over_tiles(fill)
                for way in (0, 1):
                    ring_copy(way, 0, sub, way).start()

            return act

        def second(way, sub):
            def act(pslot, slot):
                ring_copy(way, 0, sub, way).wait()

                def fill(col):
                    for part in (0, 1):
                        lo = part * half
                        total = mine(pslot, slot, col, lo, half)
                        if part == way:
                            total = total + ring_in[
                                way, 0, sub, pl.ds(lo, half), pl.ds(col, tile)
                            ].astype(jnp.float32)
                        ring_out[way, sub, pl.ds(lo, half), pl.ds(col, tile)] = total.astype(
                            jnp.bfloat16
                        )

                over_tiles(fill)
                ring_copy(way, 1, sub, None).start()

            return act

        def later(way, sub, s):
            def act(pslot, slot):
                ring_copy(way, s - 1, sub, None).wait()

                def fill(col):
                    total = mine(pslot, slot, col, 0, rows) + ring_in[
                        way, (s - 1) % 4, sub, :, pl.ds(col, tile)
                    ].astype(jnp.float32)
                    ring_out[way, sub, :, pl.ds(col, tile)] = total.astype(jnp.bfloat16)

                over_tiles(fill)
                ring_copy(way, s, sub, None).start()

            return act

        group([(h, sub, sub, first(sub)) for sub in (0, 1)], w)

        @pl.when(w > 0)
        def _():
            last(w - 1)

        group(
            [
                ((h - 1) * (1 - 2 * way), sub, 4 + 2 * way + sub, second(way, sub))
                for way in (0, 1)
                for sub in (0, 1)
            ],
            w,
        )

        def middle(s, carry):
            group(
                [
                    (
                        (h - s) * (1 - 2 * way),
                        sub,
                        4 * (s % 2) + 2 * way + sub,
                        later(way, sub, s),
                    )
                    for way in (0, 1)
                    for sub in (0, 1)
                ],
                w,
            )
            return carry

        lax.fori_loop(2, h, middle, 0)
        return carry

    def result(w, sub):
        return pltpu.make_async_copy(
            stage.at[sub], out_hbm.at[w, :, pl.ds(sub * wide, wide)], osem.at[sub]
        )

    def last(w):
        def final(sub):
            def act(pslot, slot):
                for way in (0, 1):
                    ring_copy(way, h - 1, sub, None).wait_recv()

                @pl.when(w > 0)
                def _():
                    result(w - 1, sub).wait()

                def fill(col):
                    total = mine(pslot, slot, col, 0, rows)
                    for way in (0, 1):
                        total = total + ring_in[
                            way, (h - 1) % 4, sub, :, pl.ds(col, tile)
                        ].astype(jnp.float32)
                    stage[sub, :, pl.ds(col, tile)] = total

                over_tiles(fill)
                result(w, sub).start()

            return act

        group([(0, sub, 2 + sub, final(sub)) for sub in (0, 1)], w)

    lax.fori_loop(0, count, weight, 0)
    last(count - 1)
    for sub in (0, 1):
        for way in (0, 1):
            ring_copy(way, h - 1, sub, None).wait_send()
        result(count - 1, sub).wait()


def scatter_gradients(left, right, n):
    count, length, width = right.shape
    rows = left.shape[1] // (2 * n)
    wide = width // 2
    dma = pltpu.SemaphoreType.DMA
    bf, f32 = jnp.bfloat16, jnp.float32
    return pl.pallas_call(
        functools.partial(scatter_kernel, n),
        out_shape=jax.ShapeDtypeStruct((count, rows, width), f32),
        in_specs=[pl.BlockSpec(memory_space=pl.ANY)] * 2,
        out_specs=pl.BlockSpec(memory_space=pl.ANY),
        scratch_shapes=[
            pltpu.VMEM(left.shape, bf),
            pltpu.VMEM(right.shape, bf),
            pltpu.VMEM((2, 2 * rows, wide), f32),
            pltpu.VMEM((2, rows, wide), bf),
            pltpu.VMEM((8, rows, wide), bf),
            pltpu.VMEM((2, 4, 2, rows, wide), bf),
            pltpu.VMEM((2, 2, rows, wide), bf),
            pltpu.VMEM((2, rows, wide), f32),
            dma((4,)),
            dma((4,)),
            dma((2,)),
            dma((8,)),
            dma((2, 2)),
            dma((2, 4, 2)),
            dma((2,)),
        ],
        compiler_params=pltpu.CompilerParams(
            collective_id=1, has_side_effects=True, vmem_limit_bytes=56 * 1024 * 1024
        ),
        name="scatter_gradients",
    )(left, right)


def both(own):
    return jnp.concatenate([own, lax.ppermute(own, "tensor", SWAP)], axis=0)


def reduce_rows(part):
    rows = part.shape[0] // 2
    other = lax.ppermute(part[rows:].astype(jnp.bfloat16), "tensor", SWAP)
    return part[:rows] + other.astype(jnp.float32)


def doc_positions(segment_row):
    length = segment_row.shape[0]
    indices = jnp.arange(length, dtype=jnp.int32)
    change = jnp.concatenate([jnp.ones((1,), jnp.bool_), segment_row[1:] != segment_row[:-1]])
    begins = lax.cummax(jnp.where(change, indices, 0), axis=0)
    return indices - begins


def rope_tables(positions):
    halfway = HEAD_DIM // 2
    inverse = rope_theta ** (-(jnp.arange(halfway, dtype=jnp.float32) * 2.0) / HEAD_DIM)
    angles = positions.astype(jnp.float32)[:, None] * inverse[None, :]
    return (jnp.cos(angles), jnp.sin(angles))


def rotate(field, cosine, sine_table):
    halfway = field.shape[-1] // 2
    first_half = field[..., :halfway]
    second = field[..., halfway:]
    cos_wide = cosine[:, None, :]
    sin_wide = sine_table[:, None, :]
    return jnp.concatenate(
        [first_half * cos_wide - second * sin_wide, second * cos_wide + first_half * sin_wide],
        axis=-1,
    )


def unrotate(field, cosine, sine_table):
    return rotate(field, cosine, -sine_table)


def norm_back(upstream, normed, factor, gain):
    scaled = upstream * gain
    return factor * (scaled - normed * jnp.mean(scaled * normed, axis=1, keepdims=True))


def attention_scores(queries_r, keys_r, allowed):
    scores = jnp.einsum(
        "qhd,khd->hqk", queries_r, keys_r, preferred_element_type=jnp.float32
    ) * HEAD_DIM ** (-0.5)
    return jnp.where(allowed[None], scores, masked_score)


def product(left, right):
    return jnp.dot(left, right, preferred_element_type=jnp.float32)


def product_t(left, right):
    return lax.dot_general(
        left, right, (((1,), (1,)), ((), ())), preferred_element_type=jnp.float32
    )


def body(
    n,
    tokens,
    segment_ids,
    w_query,
    w_key,
    w_value,
    w_out,
    w_gate,
    w_up,
    w_down,
    gain_query,
    gain_key,
    gain_attn,
    gain_ffn,
    cotangent,
):
    width = w_query.shape[1]
    shards = jnp.stack(
        [
            jnp.concatenate([w_query, w_key, w_value, w_out.T], axis=1),
            w_gate,
            w_up,
            w_down.T,
        ]
    )
    gathered = both(tokens)
    gains = lax.all_gather(
        jnp.stack([gain_query, gain_key, gain_attn, gain_ffn]), "fsdp", axis=1, tiled=True
    ).astype(jnp.float32)
    weights = gather_weights(shards, n)
    D = gains.shape[1]
    weights = weights.reshape(4, D, shards.shape[2])
    query_full = weights[0, :, :width]
    key_full = weights[0, :, width : 2 * width]
    value_full = weights[0, :, 2 * width : 3 * width]
    out_t = weights[0, :, 3 * width :]
    gate_full, up_full, down_t = weights[1], weights[2], weights[3]

    rank = lax.axis_index("tensor")
    heads_here = width // HEAD_DIM
    start_col = rank * width
    gain_query_here = lax.dynamic_slice_in_dim(gains[0], start_col, width)
    gain_key_here = lax.dynamic_slice_in_dim(gains[1], start_col, width)
    attn_gain_f = gains[2]
    ffn_gain_f = gains[3]
    length = gathered.shape[0]
    rows = length // 2
    segment_row = segment_ids[0]

    def arrange(row):
        flat = lax.dynamic_slice_in_dim(jnp.concatenate([row, row]), rank * rows, length)
        return flat

    indices = arrange(jnp.arange(length, dtype=jnp.int32))
    positions = arrange(doc_positions(segment_row))
    segments = arrange(segment_row)
    cosine, sine_table = rope_tables(positions)
    allowed = (segments[:, None] == segments[None, :]) & (indices[:, None] >= indices[None, :])

    queries = product(gathered, query_full)
    key_rows = product(gathered, key_full)
    values = product(gathered, value_full).astype(jnp.bfloat16)
    squares = jnp.stack([jnp.sum(queries * queries, axis=1), jnp.sum(key_rows * key_rows, axis=1)])
    squares = squares + jnp.roll(lax.ppermute(squares, "tensor", SWAP), rows, axis=1)
    query_factor = lax.rsqrt(squares[0] / D + epsilon_norm)[:, None]
    key_factor = lax.rsqrt(squares[1] / D + epsilon_norm)[:, None]
    query_hat = queries * query_factor
    key_hat = key_rows * key_factor
    queries_r = rotate(
        (query_hat * gain_query_here).reshape(length, heads_here, HEAD_DIM), cosine, sine_table
    ).astype(jnp.bfloat16)
    keys_r = rotate(
        (key_hat * gain_key_here).reshape(length, heads_here, HEAD_DIM), cosine, sine_table
    ).astype(jnp.bfloat16)
    values_r = values.reshape(length, heads_here, HEAD_DIM)
    scores = attention_scores(queries_r, keys_r, allowed)
    top_score = jnp.max(scores, axis=-1, keepdims=True)
    log_total = top_score + jnp.log(jnp.sum(jnp.exp(scores - top_score), axis=-1, keepdims=True))
    attn_probs = jnp.exp(scores - log_total).astype(jnp.bfloat16)
    attended = (
        jnp.einsum("hqk,khd->qhd", attn_probs, values_r, preferred_element_type=jnp.float32)
        .astype(jnp.bfloat16)
        .reshape(length, width)
    )
    attn_rows = reduce_rows(product_t(attended, out_t))
    attn_factor = lax.rsqrt(jnp.mean(attn_rows * attn_rows, axis=1) + epsilon_norm)[:, None]
    attn_hat = attn_rows * attn_factor
    middle = tokens.astype(jnp.float32) + attn_hat * attn_gain_f
    middle_all = both(middle.astype(jnp.bfloat16))
    gate_pre = product(middle_all, gate_full)
    up_proj = product(middle_all, up_full)
    sigmoid_gate = jax.nn.sigmoid(gate_pre)
    silu_gate = gate_pre * sigmoid_gate
    hidden = (silu_gate * up_proj).astype(jnp.bfloat16)
    down_rows = reduce_rows(product_t(hidden, down_t))
    down_factor = lax.rsqrt(jnp.mean(down_rows * down_rows, axis=1) + epsilon_norm)[:, None]
    down_hat = down_rows * down_factor
    layer_out = (middle + down_hat * ffn_gain_f).astype(jnp.bfloat16)

    grad_out = cotangent.astype(jnp.float32)
    ffn_gain_grad = jnp.sum(grad_out * down_hat, axis=0)
    grad_down = norm_back(grad_out, down_hat, down_factor, ffn_gain_f).astype(jnp.bfloat16)
    grad_down_all = both(grad_down)
    grad_hidden = product(grad_down_all, down_t)
    grad_gate = (
        grad_hidden * up_proj * sigmoid_gate * (1.0 + gate_pre * (1.0 - sigmoid_gate))
    ).astype(jnp.bfloat16)
    grad_up = (grad_hidden * silu_gate).astype(jnp.bfloat16)
    grad_middle = grad_out + reduce_rows(
        product_t(grad_gate, gate_full) + product_t(grad_up, up_full)
    )
    attn_gain_grad = jnp.sum(grad_middle * attn_hat, axis=0)
    grad_attn = norm_back(grad_middle, attn_hat, attn_factor, attn_gain_f).astype(jnp.bfloat16)
    grad_attn_all = both(grad_attn)
    grad_attended = (
        product(grad_attn_all, out_t).astype(jnp.bfloat16).reshape(length, heads_here, HEAD_DIM)
    )
    probs_again = jnp.exp(attention_scores(queries_r, keys_r, allowed) - log_total)
    grad_values = jnp.einsum(
        "hqk,qhd->khd",
        probs_again.astype(jnp.bfloat16),
        grad_attended,
        preferred_element_type=jnp.float32,
    ).astype(jnp.bfloat16)
    grad_probs = jnp.einsum(
        "qhd,khd->hqk", grad_attended, values_r, preferred_element_type=jnp.float32
    )
    grad_scores = (
        probs_again * (grad_probs - jnp.sum(probs_again * grad_probs, axis=-1, keepdims=True))
    ).astype(jnp.bfloat16)
    score_scale = HEAD_DIM ** (-0.5)
    grad_queries_r = (
        jnp.einsum("hqk,khd->qhd", grad_scores, keys_r, preferred_element_type=jnp.float32)
        * score_scale
    )
    grad_keys_r = (
        jnp.einsum("hqk,qhd->khd", grad_scores, queries_r, preferred_element_type=jnp.float32)
        * score_scale
    )
    grad_query_n = unrotate(grad_queries_r, cosine, sine_table).reshape(length, width)
    grad_key_n = unrotate(grad_keys_r, cosine, sine_table).reshape(length, width)
    query_gain_part = jnp.sum(grad_query_n * query_hat, axis=0)
    key_gain_part = jnp.sum(grad_key_n * key_hat, axis=0)
    query_scaled = grad_query_n * gain_query_here
    key_scaled = grad_key_n * gain_key_here
    dots = jnp.stack(
        [jnp.sum(query_scaled * query_hat, axis=1), jnp.sum(key_scaled * key_hat, axis=1)]
    )
    dots = dots + jnp.roll(lax.ppermute(dots, "tensor", SWAP), rows, axis=1)
    grad_queries = (query_factor * (query_scaled - query_hat * (dots[0] / D)[:, None])).astype(
        jnp.bfloat16
    )
    grad_keys = (key_factor * (key_scaled - key_hat * (dots[1] / D)[:, None])).astype(jnp.bfloat16)
    grad_values_flat = grad_values.reshape(length, width)
    grads_qkv = jnp.concatenate([grad_queries, grad_keys, grad_values_flat], axis=1)
    grad_input = grad_middle + reduce_rows(product_t(grads_qkv, weights[0, :, : 3 * width]))

    zeros = jnp.zeros((D,), jnp.float32)
    gain_parts = jnp.stack(
        [
            lax.dynamic_update_slice_in_dim(zeros, query_gain_part, start_col, 0),
            lax.dynamic_update_slice_in_dim(zeros, key_gain_part, start_col, 0),
            attn_gain_grad,
            ffn_gain_grad,
        ]
    )
    gain_sums = lax.psum(gain_parts, ("fsdp", "tensor"))
    share = D // (2 * n)
    gain_grads = lax.dynamic_slice_in_dim(gain_sums, lax.axis_index("fsdp") * share, share, axis=1)

    left = jnp.stack([grad_down_all.T, middle_all.T, gathered.T, grad_attn_all.T])
    right = jnp.stack(
        [hidden, grad_up, grad_gate, jnp.concatenate([grads_qkv, attended], axis=1)]
    )
    grads = scatter_gradients(left, right, n)
    first = grads[3]
    return (
        layer_out,
        grad_input,
        first[:, :width],
        first[:, width : 2 * width],
        first[:, 2 * width : 3 * width],
        first[:, 3 * width :].T,
        grads[2],
        grads[1],
        grads[0].T,
        gain_grads[0],
        gain_grads[1],
        gain_grads[2],
        gain_grads[3],
    )


def solution(mesh):
    rows, cols, gain = P("fsdp", "tensor"), P("tensor", "fsdp"), P("fsdp")
    acts = P(("fsdp", "tensor"), None)
    return jax.shard_map(
        functools.partial(body, mesh.shape["fsdp"] // 2),
        mesh=mesh,
        in_specs=(acts, P("fsdp", None), rows, rows, rows, cols, rows, rows, cols)
        + (gain,) * 4
        + (acts,),
        out_specs=(acts, acts, rows, rows, rows, cols, rows, rows, cols) + (gain,) * 4,
        check_vma=False,
    )
```

time: 2970 us -> 1130 us (0.38)
  waiting for transfers between devices: 2520 us -> 62.3 us
  Pallas kernels: 0 us -> 684 us
  blocking collectives: 151 us -> 62 us
  matrix products: 216 us -> 131 us
  local copies, waits for them, and re-layouts: 25.6 us -> 109 us
    reduce_scatter x11 -> x0, waiting for transfers between devices: 1400 us -> none  [the longest x1 337 us: body(): lax.psum_scatter(gate_grad, 'fsdp', scatter_dimension=0, tiled=True)]
    all_gather x18 -> x0, waiting for transfers between devices: 1120 us -> none  [the longest x2 247 us: fetch_weights(): lax.all_gather(shards[10], 'fsdp', axis=1, tiled=True)]
    pallas_call x0 -> x2, Pallas kernels: none -> 684 us  [the longest x1 349 us: gather_weights(): pl.pallas_call(functools.partial(gather_kernel, n), out_shape=jax.ShapeDt...]
    dot_general x21 -> x7, matrix products: 204 us -> 61.6 us  [product(): return jnp.dot(left, right, preferred_element_type=jnp.float32)]
    ppermute x0 -> x10, waiting for transfers between devices: none -> 62.3 us  [the longest x4 42.3 us: reduce_rows(): other = lax.ppermute(part[rows:].astype(jnp.bfloat16), 'tensor', SWAP)]
    unnamed x1 -> x0, blocking collectives: 60.5 us -> none
    all_gather x4 -> x1, blocking collectives: 77.9 us -> 21.6 us  [body(): lax.all_gather(jnp.stack([gain_query, gain_key, gain_attn, gain_ffn]), 'f...]
    dot_general x0 -> x5, matrix products: none -> 54.9 us  [product_t(): lax.dot_general(left, right, (((1,), (1,)), ((), ())), preferred_element_...]
  transfers between devices with their start and end apart: 29 -> 10, of which waited for: 26 -> 5; matrix products, arithmetic and copies ran while one was open for 7% -> 9% of each run, Pallas kernels for 0% -> 61%
where the time goes in v1:
time: 1130 us; the launch traced here: 1120 us
  Pallas kernels  684 us (61%)
  matrix products  131 us (12%)
  local copies, waits for them, and re-layouts  109 us (10%)
  waiting for transfers between devices  62.3 us (6%)
  blocking collectives  62 us (5%)
  other arithmetic  60.7 us (5%)
  starting transfers between devices  13.3 us (1%)
    pallas_call x1, Pallas kernels, gather_weights(): pl.pallas_call(functools.partial(gather_kernel, n), out_shape=jax.ShapeDt...  349 us
    pallas_call x1, Pallas kernels, scatter_gradients(): pl.pallas_call(functools.partial(scatter_kernel, n), out_shape=jax.ShapeD...  335 us
    dot_general x7, matrix products, product(): return jnp.dot(left, right, preferred_element_type=jnp.float32)  61.6 us
    dot_general x5, matrix products, product_t(): lax.dot_general(left, right, (((1,), (1,)), ((), ())), preferred_element_...  54.9 us
    ppermute x4, waiting for transfers between devices, reduce_rows(): other = lax.ppermute(part[rows:].astype(jnp.bfloat16), 'tensor', SWAP)  42.3 us
    psum x1, blocking collectives, body(): gain_sums = lax.psum(gain_parts, ('fsdp', 'tensor'))  40.4 us
    slice x1, local copies, waits for them, and re-layouts, body(): gate_full, up_full, down_t = (weights[1], weights[2], weights[3])  32.7 us
    unnamed x151, local copies, waits for them, and re-layouts  29.8 us
  transfers between devices with their start and end apart: 10, of which 5 were waited for; matrix products, arithmetic and copies ran while one was open for 9% of the time, Pallas kernels for 61%

profile of v1, /device:TPU:0, one launch (start us, length us, event | category | flops | bytes accessed | tf_op | source)
XLA Modules:
  0.0 1123.7 jit_solution(7719401853165168963)
XLA Ops:
  0.7 3.0 collective-permute-start
  8.3 21.6 %all_gather.3 = bf16[4,2048]{1,0:T(4,128)(2,1)S(1)} all-gather(bf16[4,128]{1,0:T(4,128)(2,1)S(1)} %pad_maximum_fusion.18), channel_id=1, replica_groups=mesh['fsdp'=16,'tensor'=2] {'fsdp'}, dimensions={1}, use_global_device_ids=true | all-gather | bytes 17408 | tf_op jit(solution)/shard_map/all_gather | solution.py:567
  34.7 349.2 %gather_weights.1 = bf16[4,16,128,4096]{3,2,1,0:T(8,128)(2,1)} custom-call(bf16[4,128,4096]{2,1,0:T(8,128)(2,1)} %pad_maximum_fusion.2.w_ref), custom_call_target="tpu_custom_call" | custom-call | tf_op jit(solution)/shard_map/gather_weights/pallas_call | solution.py:188
  387.4 4.5 multiply_reduce_fusion.7
  392.0 4.7 multiply_reduce_fusion.8
  397.4 4.1 fusion.24
  410.8 4.3 fusion.6
  418.8 16.4 %collective-permute-done.2 = bf16[192,2048]{1,0:T(8,128)(2,1)} collective-permute-done((bf16[192,2048]{1,0:T(8,128)(2,1)S(1)}, bf16[192,2048]{1,0:T(8,128)(2,1)}, u32[]{:S(2)}, u32[]{:S(2)}) %collective-permute-start.2) | collective-permute-done | bytes 786464 | tf_op jit(solution)/shard_map/ppermute | solution.py:483
  441.8 32.7 %fusion.56 = (bf16[1,16,128,4096]{3,2,1,0:T(8,128)(2,1)}, bf16[1,16,128,4096]{3,2,1,0:T(8,128)(2,1)}, bf16[1,16,128,4096]{3,2,1,0:T(8,128)(2,1)}) fusion(bf16[4,16,128,4096]{3,2,1,0:T(8,128)(2,1)} %gather_weights.1), kind=kLoop, calls=%fused_computation.166 | loop fusion | bytes 100663296 | tf_op jit(solution)/shard_map/slice | solution.py:577
  476.7 13.3 %fusion.54 = f32[384,4096]{1,0:T(8,128)S(1)} fusion(bf16[2048,4096]{1,0:T(8,128)(2,1)} %bitcast.165, bf16[192,2048]{0,1:T(8,128)(2,1)} %copy.118, bf16[192,2048]{0,1:T(8,128)(2,1)S(1)} %fusion.25), kind=kOutput, calls=%fused_computation.164 | convolution fusion | flops 6445596672 | bytes 24641536 | tf_op jit(solution)/shard_map/dot_general | solution.py:531
  490.0 15.5 %multiply_convert_fusion.2 = (bf16[384,4096]{1,0:T(8,128)(2,1)S(1)}, f32[384,4096]{1,0:T(8,128)}) fusion(f32[384,4096]{1,0:T(8,128)S(1)} %fusion.54, bf16[2048,4096]{1,0:T(8,128)(2,1)} %bitcast.167, bf16[192,2048]{0,1:T(8,128)(2,1)S(1)} %copy-done.17, bf16[192,2048]{0,1:T(8,128)(2,1)S(1)} %fusion.25), kind=kOutput, calls=%fused_computation.6 | convolution fusion | flops 6455033856 | bytes 34078720 | tf_op jit(solution)/shard_map/dot_general | solution.py:531
  505.5 11.8 %fusion.62 = f32[384,2048]{1,0:T(8,128)S(1)} fusion(bf16[384,4096]{1,0:T(8,128)(2,1)S(1)} %get-tuple-element.119, bf16[2048,4096]{1,0:T(8,128)(2,1)} %bitcast.169), kind=kOutput, calls=%fused_computation.172 | convolution fusion | flops 6442450944 | bytes 23068672 | tf_op jit(solution)/shard_map/dot_general | solution.py:535
  527.7 10.3 collective-permute-done.4
  550.8 16.8 %collective-permute-done.5 = bf16[192,2048]{1,0:T(8,128)(2,1)} collective-permute-done((bf16[192,2048]{1,0:T(8,128)(2,1)}, bf16[192,2048]{1,0:T(8,128)(2,1)}, u32[]{:S(2)}, u32[]{:S(2)}) %collective-permute-start.5) | collective-permute-done | bytes 786464 | tf_op jit(solution)/shard_map/ppermute | solution.py:478
  569.8 15.4 %multiply_convert_fusion = (bf16[384,4096]{1,0:T(8,128)(2,1)S(1)}, bf16[384,4096]{1,0:T(8,128)(2,1)S(1)}) fusion(f32[384,4096]{1,0:T(8,128)} %copy-done.29, f32[384,4096]{1,0:T(8,128)} %get-tuple-element.120, bf16[2048,4096]{1,0:T(8,128)(2,1)} %bitcast.170, bf16[192,2048]{0,1:T(8,128)(2,1)} %copy.123, bf16[192,2048]{0,1:T(8,128)(2,1)} %get-tuple-element.80), kind=kOutput, calls=%fused_computation.4 | convolution fusion | flops 6466043904 | bytes 37224448 | tf_op jit(solution)/shard_map/dot_general | solution.py:531
  585.2 14.3 %fusion.63 = f32[384,2048]{0,1:T(8,128)S(1)} fusion(bf16[384,4096]{1,0:T(8,128)(2,1)S(1)} %get-tuple-element.71, bf16[2048,4096]{1,0:T(8,128)(2,1)} %bitcast.166), kind=kOutput, calls=%fused_computation.173 | convolution fusion | flops 6442450944 | bytes 23068672 | tf_op jit(solution)/shard_map/dot_general | solution.py:535
  599.6 12.5 %convolution_add_fusion = f32[384,2048]{0,1:T(8,128)S(1)} fusion(f32[384,2048]{0,1:T(8,128)S(1)} %fusion.63, bf16[384,4096]{1,0:T(8,128)(2,1)S(1)} %get-tuple-element.70, bf16[2048,4096]{1,0:T(8,128)(2,1)} %bitcast.168), kind=kOutput, calls=%fused_computation.29 | convolution fusion | flops 6443237376 | bytes 26214400 | tf_op jit(solution)/shard_map/dot_general | solution.py:535
  618.5 15.7 %collective-permute-done.6 = bf16[192,2048]{1,0:T(8,128)(2,1)} collective-permute-done((bf16[192,2048]{1,0:T(8,128)(2,1)}, bf16[192,2048]{1,0:T(8,128)(2,1)}, u32[]{:S(2)}, u32[]{:S(2)}) %collective-permute-start.6) | collective-permute-done | bytes 786464 | tf_op jit(solution)/shard_map/ppermute | solution.py:483
  636.4 3.1 multiply_reduce_fusion.1
  654.4 3.1 fusion.30
  657.5 3.1 collective-permute-done.7
  662.2 4.1 fusion.22
  668.6 4.8 convolution_convert_fusion
  673.3 3.8 multiply_reduce_fusion
  686.2 40.4 %psum.7 = f32[4,2048]{1,0:T(4,128)S(1)} all-reduce(f32[4,2048]{1,0:T(4,128)S(1)} %pad_maximum_fusion.15), channel_id=1, replica_groups=mesh['fsdp'=16,'tensor'=2] {'fsdp','tensor'}, use_global_device_ids=true, to_apply=%region_17.18 | all-reduce | flops 8192 | bytes 65536 | tf_op jit(solution)/shard_map/psum | solution.py:707
  729.0 6.6 pad_maximum_fusion.1.left_hbm
  738.6 4.1 multiply_convert_fusion.5
  744.5 11.9 %fusion = f32[384,2048]{1,0:T(8,128)} fusion(bf16[4,2048,4096]{2,1,0:T(8,128)(2,1)} %bitcast.6, bf16[384,1024]{1,0:T(8,128)(2,1)S(1)} %copy-done.42, bf16[384,1024]{1,0:T(8,128)(2,1)} %multiply_convert_fusion.5, bf16[384,1024]{1,0:T(8,128)(2,1)} %multiply_convert_fusion.6), kind=kOutput, calls=%fused_computation.1 | convolution fusion | flops 4838916096 | bytes 18087936 | tf_op jit(solution)/shard_map/dot_general | solution.py:535
  759.7 5.6 pad_maximum_fusion.right_hbm
  765.3 334.8 %scatter_gradients.1 = f32[4,128,4096]{2,1,0:T(8,128)} custom-call(bf16[4,2048,384]{2,1,0:T(8,128)(2,1)} %pad_maximum_fusion.1.left_hbm, bf16[4,384,4096]{2,1,0:T(8,128)(2,1)} %pad_maximum_fusion.right_hbm), custom_call_target="tpu_custom_call" | custom-call | tf_op jit(solution)/shard_map/scatter_gradients/pallas_call | solution.py:448
  1100.1 6.5 slice_bitcast_fusion.11
  1117.2 3.3 add_add_fusion
  (261 shorter events, 120.0 us)
Async XLA Ops:
  0.6 29.4 %copy-start.56 = (bf16[1024,128]{1,0:T(8,128)(2,1)S(1)}, bf16[1024,128]{1,0:T(8,128)(2,1)}, u32[]{:S(2)}) copy-start(bf16[1024,128]{1,0:T(8,128)(2,1)} %param.19) | copy-start | bytes 786436
  0.7 29.5 %copy-start.49 = (bf16[4096,128]{1,0:T(8,128)(2,1)S(1)}, bf16[4096,128]{1,0:T(8,128)(2,1)}, u32[]{:S(2)}) copy-start(bf16[4096,128]{1,0:T(8,128)(2,1)} %param.22) | copy-start | bytes 3145732
  0.7 385.1 %collective-permute-start = (bf16[192,2048]{1,0:T(8,128)(2,1)}, bf16[192,2048]{1,0:T(8,128)(2,1)}, u32[]{:S(2)}, u32[]{:S(2)}) collective-permute-start(bf16[192,2048]{1,0:T(8,128)(2,1)} %param.14), channel_id=1, source_target_pairs={{0,1},{1,0},{2,3},{3,2},{4,5},{5,4},{6,7},{7,6},{8,9},{9,8},{10,11... | collective-permute-start | bytes 2359304 | tf_op jit(solution)/shard_map/ppermute | solution.py:478
  5.2 392.2 %copy-start.4 = (bf16[192,2048]{0,1:T(8,128)(2,1)}, bf16[192,2048]{0,1:T(8,128)(2,1)S(1)}, u32[]{:S(2)}) copy-start(bf16[192,2048]{0,1:T(8,128)(2,1)S(1)} %copy.103) | copy-start | bytes 2359300
  384.1 17.6 %copy-start.59 = (f32[1,1024]{1,0:T(1,128)}, f32[1,1024]{1,0:T(1,128)S(1)}, u32[]{:S(2)}) copy-start(f32[1,1024]{1,0:T(1,128)S(1)} %get-tuple-element.124) | copy-start | bytes 12292
  384.1 18.3 %copy-start.61 = (f32[1,1024]{1,0:T(1,128)}, f32[1,1024]{1,0:T(1,128)S(1)}, u32[]{:S(2)}) copy-start(f32[1,1024]{1,0:T(1,128)S(1)} %get-tuple-element.123) | copy-start | bytes 12292
  384.3 23.7 %copy-start.32 = (pred[384,384]{0,1:T(8,128)(4,1)}, pred[384,384]{0,1:T(8,128)(4,1)S(1)}, u32[]{:S(2)}) copy-start(pred[384,384]{0,1:T(8,128)(4,1)S(1)} %compare_and_fusion) | copy-start | bytes 442372
  385.7 18.2 %copy-start.47 = (f32[384,64]{1,0:T(8,128)}, f32[384,64]{1,0:T(8,128)S(1)}, u32[]{:S(2)}) copy-start(f32[384,64]{1,0:T(8,128)S(1)} %get-tuple-element.108) | copy-start | bytes 294916
  387.4 9.9 copy-start.30
  392.0 10.4 copy-start.15
  396.8 4.7 collective-permute-start.1
  415.2 19.9 %collective-permute-start.2 = (bf16[192,2048]{1,0:T(8,128)(2,1)S(1)}, bf16[192,2048]{1,0:T(8,128)(2,1)}, u32[]{:S(2)}, u32[]{:S(2)}) collective-permute-start(bf16[192,2048]{1,0:T(8,128)(2,1)S(1)} %slice.324), channel_id=1, source_target_pairs={{0,1},{1,0},{2,3},{3,2},{4,5},{5,4},{6,7},{7,6},{8,9},{9,8},{10,11... | collective-permute-start | bytes 2359304 | tf_op jit(solution)/shard_map/ppermute | solution.py:483
  440.5 34.0 %collective-permute-start.3 = (bf16[192,2048]{1,0:T(8,128)(2,1)}, bf16[192,2048]{1,0:T(8,128)(2,1)}, u32[]{:S(2)}, u32[]{:S(2)}) collective-permute-start(bf16[192,2048]{1,0:T(8,128)(2,1)} %copy.117), channel_id=1, source_target_pairs={{0,1},{1,0},{2,3},{3,2},{4,5},{5,4},{6,7},{7,6},{8,9},{9,8},{10,11... | collective-permute-start | bytes 2359304 | tf_op jit(solution)/shard_map/ppermute | solution.py:478
  476.7 13.3 %copy-start.17 = (bf16[192,2048]{0,1:T(8,128)(2,1)S(1)}, bf16[192,2048]{0,1:T(8,128)(2,1)}, u32[]{:S(2)}) copy-start(bf16[192,2048]{0,1:T(8,128)(2,1)} %copy.118) | copy-start | bytes 2359300
  490.0 15.5 %copy-start.29 = (f32[384,4096]{1,0:T(8,128)}, f32[384,4096]{1,0:T(8,128)S(1)}, u32[]{:S(2)}) copy-start(f32[384,4096]{1,0:T(8,128)S(1)} %fusion.54) | copy-start | bytes 18874372
  505.5 11.9 %copy-start.34 = (bf16[384,4096]{1,0:T(8,128)(2,1)}, bf16[384,4096]{1,0:T(8,128)(2,1)S(1)}, u32[]{:S(2)}) copy-start(bf16[384,4096]{1,0:T(8,128)(2,1)S(1)} %get-tuple-element.119) | copy-start | bytes 9437188
  519.3 18.7 %collective-permute-start.4 = (bf16[192,2048]{1,0:T(8,128)(2,1)}, bf16[192,2048]{1,0:T(8,128)(2,1)}, u32[]{:S(2)}, u32[]{:S(2)}) collective-permute-start(bf16[192,2048]{1,0:T(8,128)(2,1)} %slice.323), channel_id=1, source_target_pairs={{0,1},{1,0},{2,3},{3,2},{4,5},{5,4},{6,7},{7,6},{8,9},{9,8},{10,11... | collective-permute-start | bytes 2359304 | tf_op jit(solution)/shard_map/ppermute | solution.py:483
  549.8 17.8 %collective-permute-start.5 = (bf16[192,2048]{1,0:T(8,128)(2,1)}, bf16[192,2048]{1,0:T(8,128)(2,1)}, u32[]{:S(2)}, u32[]{:S(2)}) collective-permute-start(bf16[192,2048]{1,0:T(8,128)(2,1)} %copy.122), channel_id=1, source_target_pairs={{0,1},{1,0},{2,3},{3,2},{4,5},{5,4},{6,7},{7,6},{8,9},{9,8},{10,11... | collective-permute-start | bytes 2359304 | tf_op jit(solution)/shard_map/ppermute | solution.py:478
  585.2 14.3 %copy-start.38 = (bf16[384,4096]{1,0:T(8,128)(2,1)}, bf16[384,4096]{1,0:T(8,128)(2,1)S(1)}, u32[]{:S(2)}) copy-start(bf16[384,4096]{1,0:T(8,128)(2,1)S(1)} %get-tuple-element.71) | copy-start | bytes 9437188
  585.2 14.3 %copy-start.36 = (bf16[384,4096]{1,0:T(8,128)(2,1)}, bf16[384,4096]{1,0:T(8,128)(2,1)S(1)}, u32[]{:S(2)}) copy-start(bf16[384,4096]{1,0:T(8,128)(2,1)S(1)} %get-tuple-element.70) | copy-start | bytes 9437188
  617.3 16.9 %collective-permute-start.6 = (bf16[192,2048]{1,0:T(8,128)(2,1)}, bf16[192,2048]{1,0:T(8,128)(2,1)}, u32[]{:S(2)}, u32[]{:S(2)}) collective-permute-start(bf16[192,2048]{1,0:T(8,128)(2,1)} %copy.126), channel_id=1, source_target_pairs={{0,1},{1,0},{2,3},{3,2},{4,5},{5,4},{6,7},{7,6},{8,9},{9,8},{10,11... | collective-permute-start | bytes 2359304 | tf_op jit(solution)/shard_map/ppermute | solution.py:483
  644.6 6.8 copy-start.18
  644.6 15.9 %collective-permute-start.7 = (bf16[192,2048]{1,0:T(8,128)(2,1)}, bf16[192,2048]{1,0:T(8,128)(2,1)}, u32[]{:S(2)}, u32[]{:S(2)}) collective-permute-start(bf16[192,2048]{1,0:T(8,128)(2,1)} %copy.128), channel_id=1, source_target_pairs={{0,1},{1,0},{2,3},{3,2},{4,5},{5,4},{6,7},{7,6},{8,9},{9,8},{10,11... | collective-permute-start | bytes 2359304 | tf_op jit(solution)/shard_map/ppermute | solution.py:478
  654.4 7.8 copy-start.19
  668.5 8.6 slice-start
  726.7 11.8 %collective-permute-start.8 = (f32[2,384]{1,0:T(2,128)S(1)}, f32[2,384]{1,0:T(2,128)S(1)}, u32[]{:S(2)}, u32[]{:S(2)}) collective-permute-start(f32[2,384]{1,0:T(2,128)S(1)} %pad_maximum_fusion.17), channel_id=1, source_target_pairs={{0,1},{1,0},{2,3},{3,2},{4,5},{5,4},{6,7},{7,6},{8,9},{9,8},{10,11... | collective-permute-start | bytes 9224 | tf_op jit(solution)/shard_map/ppermute | solution.py:689
  744.4 12.0 %copy-start.41 = (bf16[384,1024]{1,0:T(8,128)(2,1)S(1)}, bf16[384,1024]{1,0:T(8,128)(2,1)}, u32[]{:S(2)}) copy-start(bf16[384,1024]{1,0:T(8,128)(2,1)} %copy.159) | copy-start | bytes 2359300
  744.4 12.0 %copy-start.43 = (bf16[384,1024]{1,0:T(8,128)(2,1)S(1)}, bf16[384,1024]{1,0:T(8,128)(2,1)}, u32[]{:S(2)}) copy-start(bf16[384,1024]{1,0:T(8,128)(2,1)} %multiply_convert_fusion.5) | copy-start | bytes 2359300
  744.4 12.0 %copy-start.44 = (bf16[384,1024]{1,0:T(8,128)(2,1)S(1)}, bf16[384,1024]{1,0:T(8,128)(2,1)}, u32[]{:S(2)}) copy-start(bf16[384,1024]{1,0:T(8,128)(2,1)} %multiply_convert_fusion.6) | copy-start | bytes 2359300
  744.5 14.1 %copy-start.39 = (bf16[384,4096]{1,0:T(8,128)(2,1)S(1)}, bf16[384,4096]{1,0:T(8,128)(2,1)}, u32[]{:S(2)}) copy-start(bf16[384,4096]{1,0:T(8,128)(2,1)} %copy-done.38) | copy-start | bytes 9437188
  758.4 357.4 %collective-permute-start.9 = (bf16[192,2048]{1,0:T(8,128)(2,1)S(1)}, bf16[192,2048]{1,0:T(8,128)(2,1)}, u32[]{:S(2)}, u32[]{:S(2)}) collective-permute-start(bf16[192,2048]{1,0:T(8,128)(2,1)S(1)} %slice.322), channel_id=1, source_target_pairs={{0,1},{1,0},{2,3},{3,2},{4,5},{5,4},{6,7},{7,6},{8,9},{9,8},{10,11... | collective-permute-start | bytes 2359304 | tf_op jit(solution)/shard_map/ppermute | solution.py:483
  1100.1 6.5 copy-start.45
  (47 other events, 104.6 us)

commit v2 on v1

--- a/solution.py
+++ b/solution.py
@@ -42,15 +42,16 @@
         self.next = (self.chip(1) * 2 + self.c, self.t)
         self.prev = (self.chip(-1) * 2 + self.c, self.t)
         self.mate = (self.f + 1 - 2 * self.c, self.t)
+        self.partner = (self.f, 1 - self.t)
 
     def chip(self, offset):
         return ring_chip((self.pos + offset + self.n) % self.n, self.n)
 
     def greet(self):
         barrier = pltpu.get_barrier_semaphore()
-        for peer in (self.next, self.prev, self.mate):
+        for peer in (self.next, self.prev, self.mate, self.partner):
             pl.semaphore_signal(barrier, inc=1, device_id=peer, device_id_type=MESH)
-        pl.semaphore_wait(barrier, 3)
+        pl.semaphore_wait(barrier, 4)
 
 
 def remote(src, dst, send, recv, peer):
@@ -64,49 +65,195 @@
     )
 
 
-def gather_kernel(n, w_ref, g_ref, ssem, rsem, msend, mrecv, osend, orecv, lsem):
+def repeat(lo, hi, fn):
+    if hi - lo <= 4:
+        for i in range(lo, hi):
+            fn(i)
+    else:
+
+        def one(i, carry):
+            fn(i)
+            return carry
+
+        lax.fori_loop(lo, hi, one, 0)
+
+
+def loop(count, fn):
+    def one(i, carry):
+        fn(i)
+        return carry
+
+    lax.fori_loop(0, count, one, 0)
+
+
+def nt_dot(left, right):
+    return lax.dot_general(
+        left, right, (((1,), (1,)), ((), ())), preferred_element_type=jnp.float32
+    )
+
+
+def nn_dot(left, right):
+    return jnp.dot(left, right, preferred_element_type=jnp.float32)
+
+
+class Stream:
+    def __init__(self, g_ref, wcol, wrow, sem):
+        self.g, self.wcol, self.wrow, self.sem = g_ref, wcol, wrow, sem
+
+    def cols(self, w, start, count, fn):
+        tile = self.wcol.shape[2]
+
+        def copy(j):
+            col = pl.multiple_of(start + j * tile, tile)
+            return pltpu.make_async_copy(
+                self.g.at[w, :, pl.ds(col, tile)], self.wcol.at[j % 2], self.sem.at[j % 2]
+            )
+
+        copy(0).start()
+
+        def one(j):
+            @pl.when(j + 1 < count)
+            def _():
+                copy(j + 1).start()
+
+            copy(j).wait()
+            fn(j, self.wcol.at[j % 2])
+
+        loop(count, one)
+
+    def row_copy(self, w, chunk, slot, start, width):
+        size = self.wrow.shape[1]
+        return pltpu.make_async_copy(
+            self.g.at[w, pl.ds(pl.multiple_of(chunk * size, size), size), pl.ds(start, width)],
+            self.wrow.at[slot, :, pl.ds(0, width)],
+            self.sem.at[slot],
+        )
+
+    def rows(self, w, start, width, fn):
+        count = self.g.shape[1] // self.wrow.shape[1]
+        self.row_copy(w, 0, 0, start, width).start()
+
+        def one(j):
+            @pl.when(j + 1 < count)
+            def _():
+                self.row_copy(w, j + 1, (j + 1) % 2, start, width).start()
+
+            self.row_copy(w, j, j % 2, start, width).wait()
+            fn(j, self.wrow.at[j % 2, :, pl.ds(0, width)])
+
+        loop(count, one)
+
+
+def forward_kernel(
+    n,
+    w_ref,
+    tok_ref,
+    cot_ref,
+    gain_ref,
+    cos_ref,
+    sin_ref,
+    bias_ref,
+    g_ref,
+    out_ref,
+    x_out,
+    hat_out,
+    qr_out,
+    kr_out,
+    v_out,
+    o_out,
+    ahat_out,
+    mb_out,
+    silu_out,
+    slope_out,
+    hid_out,
+    df_out,
+    fac_ref,
+    gffn_ref,
+    x,
+    cot,
+    hat,
+    qr,
+    kr,
+    v,
+    o,
+    sq,
+    sq_in,
+    part,
+    part_out,
+    part_in,
+    down_in,
+    ahat,
+    mid,
+    mb,
+    gate,
+    up,
+    silu,
+    slope,
+    hid,
+    df,
+    wcol,
+    wrow,
+    ssem,
+    rsem,
+    msend,
+    mrecv,
+    osend,
+    orecv,
+    lsem,
+    wsem,
+    ysend,
+    yrecv,
+    fsend,
+    frecv,
+    save_sem,
+):
     ring = Ring(n)
     h = ring.h
     count, rows, _ = w_ref.shape
-    half = rows // 2
+    piece_half = rows // 2
+    own_rows = tok_ref.shape[0]
+    length = 2 * own_rows
+    D = x.shape[1]
+    local = v.shape[1]
+    heads = local // HEAD_DIM
+    chunk = wrow.shape[1]
+
+    load = [
+        pltpu.make_async_copy(tok_ref, x.at[pl.ds(0, own_rows), :], lsem.at[count]),
+        pltpu.make_async_copy(cot_ref, cot.at[pl.ds(0, own_rows), :], lsem.at[count + 1]),
+    ]
+    for copy in load:
+        copy.start()
     ring.greet()
 
-    def slot(w, offset):
-        return (ring.chip(offset) * 2 + ring.c, w)
-
-    def part(ref, piece):
+    def spot(w, s):
+        return g_ref.at[w, pl.ds(pl.multiple_of(s * rows, rows), rows), :]
+
+    def cut(ref, piece):
         if piece is None:
             return ref
-        return ref.at[pl.ds(piece * half, half), :]
-
-    def hop(w, way, d, piece):
-        origin = -d if way == 0 else d
-        s, _ = slot(w, origin)
-        src = w_ref.at[w] if isinstance(d, int) and d == 0 else g_ref.at[w, s]
+        return ref.at[pl.ds(piece * piece_half, piece_half), :]
+
+    def piece_of(d, way):
+        return way if isinstance(d, int) and d == h - 1 else None
+
+    def away(way, d):
+        return ring.chip(-d if way == 0 else d) * 2
+
+    def hop(w, way, d):
+        piece = piece_of(d, way)
+        s = away(way, d) + ring.c
+        src = w_ref.at[w] if isinstance(d, int) and d == 0 else spot(w, s)
         return remote(
-            part(src, piece),
-            part(g_ref.at[w, s], piece),
+            cut(src, piece),
+            cut(spot(w, s), piece),
             ssem.at[w, way, d % 4],
             rsem.at[w, way, d % 4],
             ring.next if way == 0 else ring.prev,
         )
 
-    def share(w, way, d, piece):
-        origin = -1 - d if way == 0 else 1 + d
-        s, _ = slot(w, origin)
-        ref = part(g_ref.at[w, s], piece)
-        return remote(ref, ref, msend.at[w, way, d % 4], mrecv.at[w, way, d % 4], ring.mate)
-
-    def share_in(w, way, d, piece):
-        origin = -1 - d if way == 0 else 1 + d
-        s = ring.chip(origin) * 2 + 1 - ring.c
-        ref = part(g_ref.at[w, s], piece)
-        return remote(ref, ref, msend.at[w, way, d % 4], mrecv.at[w, way, d % 4], ring.mate)
-
-    def arrival(w, way, d, piece):
-        origin = -1 - d if way == 0 else 1 + d
-        s, _ = slot(w, origin)
-        ref = part(g_ref.at[w, s], piece)
+    def arrival(w, way, d):
+        ref = cut(spot(w, away(way, d + 1) + ring.c), piece_of(d, way))
         return remote(
             ref,
             ref,
@@ -115,93 +262,372 @@
             ring.next if way == 0 else ring.prev,
         )
 
-    def own(w):
-        return (
-            remote(w_ref.at[w], g_ref.at[w, ring.f], osend.at[w], orecv.at[w], ring.mate),
-            pltpu.make_async_copy(w_ref.at[w], g_ref.at[w, ring.f], lsem.at[w]),
-        )
+    def share(w, way, d, core):
+        ref = cut(spot(w, away(way, d + 1) + core), piece_of(d, way))
+        return remote(ref, ref, msend.at[w, way, d % 4], mrecv.at[w, way, d % 4], ring.mate)
+
+    def own_mate(w):
+        return remote(w_ref.at[w], spot(w, ring.f), osend.at[w], orecv.at[w], ring.mate)
+
+    def own_here(w):
+        return pltpu.make_async_copy(w_ref.at[w], spot(w, ring.f), lsem.at[w])
 
     def begin(w):
         for way in (0, 1):
-            hop(w, way, 0, None).start()
-        for copy in own(w):
-            copy.start()
-
-    def piece_of(d, way):
-        return way if d == h - 1 else None
+            hop(w, way, 0).start()
+        own_mate(w).start()
+        own_here(w).start()
+
+    def step(w, d):
+        for way in (0, 1):
+            arrival(w, way, d).wait_recv()
+            if not isinstance(d, int) or d < h - 1:
+                hop(w, way, d + 1).start()
+            share(w, way, d, ring.c).start()
+
+    def steps(w, lo, hi):
+        first, last = lo * h // 4, hi * h // 4
+        repeat(first, min(last, h - 2), lambda d: step(w, d))
+        for d in range(max(first, h - 2), last):
+            step(w, d)
+
+    def shared(w, lo, hi):
+        def one(d):
+            for way in (0, 1):
+                share(w, way, d, 1 - ring.c).wait_recv()
+
+        repeat(lo, min(hi, h - 1), one)
+        if hi == h:
+            one(h - 1)
+
+    def own_shared(w):
+        ref = spot(w, ring.mate[0])
+        remote(ref, ref, osend.at[w], orecv.at[w], ring.mate).wait_recv()
+        own_here(w).wait()
+
+    def complete(w):
+        own_shared(w)
+        shared(w, 0, h)
+
+    partner = (ring.f, 1 - ring.t)
+
+    def swap(i, src, dst):
+        return remote(src, dst, ysend.at[i], yrecv.at[i], partner)
+
+    low, high = pl.ds(0, own_rows), pl.ds(own_rows, own_rows)
+    swaps = [
+        swap(0, tok_ref, x.at[high, :]),
+        swap(1, cot_ref, cot.at[high, :]),
+        swap(2, sq.at[low, :], sq_in.at[high, :]),
+        swap(3, sq.at[high, :], sq_in.at[low, :]),
+        swap(4, part_out, part_in),
+    ]
+
+    def sum_copy(k, width):
+        view = pl.ds(pl.multiple_of(k * width, width), width)
+        return remote(
+            part_out.at[:, view], down_in.at[:, view], fsend.at[k], frecv.at[k], partner
+        )
+
+    saves = []
+
+    def save(src, dst):
+        copy = pltpu.make_async_copy(src, dst, save_sem.at[len(saves)])
+        copy.start()
+        saves.append(copy)
+
+    stream = Stream(g_ref, wcol, wrow, wsem)
 
     begin(0)
+    swaps[0].start()
+    swaps[1].start()
+    steps(0, 0, 1)
+    begin(1)
+    steps(0, 1, 4)
+    load[0].wait()
+    swaps[0].wait_recv()
+    save(x, x_out)
+    complete(0)
+
+    tile = wcol.shape[2]
+    lane = lax.broadcasted_iota(jnp.int32, (length, HEAD_DIM), 1)
+    sq[...] = jnp.zeros_like(sq)
+
+    def query_key(j, w):
+        acc = nn_dot(x[...], w[...])
+        hat[:, pl.ds(pl.multiple_of(j * tile, tile), tile)] = acc
+        side = (j * tile) // local
+        total = jnp.sum(acc * acc, axis=1, keepdims=True)
+        sq[...] += jnp.where(lane // (HEAD_DIM // 2) == side, total, 0.0)
+
+    def value(j, w):
+        v[:, pl.ds(pl.multiple_of(j * tile, tile), tile)] = nn_dot(x[...], w[...]).astype(
+            jnp.bfloat16
+        )
+
+    stream.cols(0, 0, 2 * local // tile, query_key)
+    swaps[2].start()
+    swaps[3].start()
+    stream.cols(0, 2 * local, local // tile, value)
+    save(v, v_out)
+    steps(1, 0, 1)
+    begin(2)
+    for i in (2, 3):
+        swaps[i].wait_recv()
+    both_sq = sq[...] + sq_in[...]
+    for i in (2, 3):
+        swaps[i].wait_send()
+    for side in (0, 1):
+        col = both_sq[:, side * (HEAD_DIM // 2) : side * (HEAD_DIM // 2) + 1]
+        fac_ref[side] = jnp.broadcast_to(
+            lax.rsqrt(col / D + epsilon_norm), (length, HEAD_DIM)
+        )
+
+    def head(i):
+        at = pl.ds(pl.multiple_of(i * HEAD_DIM, HEAD_DIM), HEAD_DIM)
+        gain_at = pl.ds(pl.multiple_of(ring.t * local + i * HEAD_DIM, HEAD_DIM), HEAD_DIM)
+        for side, dst in ((0, qr), (1, kr)):
+            where = pl.ds(pl.multiple_of(side * local + i * HEAD_DIM, HEAD_DIM), HEAD_DIM)
+            normed = hat[:, where] * fac_ref[side]
+            hat[:, where] = normed
+            scaled = normed * gain_ref[side : side + 1, gain_at]
+            turned = scaled * cos_ref[...] + pltpu.roll(scaled, HEAD_DIM // 2, 1) * sin_ref[...]
+            dst[:, at] = turned.astype(jnp.bfloat16)
+        scores = nt_dot(qr[:, at], kr[:, at]) * HEAD_DIM ** (-0.5) + bias_ref[...]
+        top = jnp.max(scores, axis=1, keepdims=True)
+        raised = jnp.exp(scores - top)
+        probs = raised / jnp.sum(raised, axis=1, keepdims=True)
+        o[:, at] = nn_dot(probs.astype(jnp.bfloat16), v[:, at]).astype(jnp.bfloat16)
+
+    loop(heads, head)
+    save(hat, hat_out)
+    save(qr, qr_out)
+    save(kr, kr_out)
+    save(o, o_out)
+    steps(1, 1, 2)
+
+    def split(k, width, acc):
+        view = pl.ds(pl.multiple_of(k * width, width), width)
+        part[:, view] = acc
+        part_out[low, view] = acc[own_rows:].astype(jnp.bfloat16)
+        part_out[high, view] = acc[:own_rows].astype(jnp.bfloat16)
+
+    stream.rows(0, 3 * local, local, lambda k, w: split(k, chunk, nt_dot(o[...], w[...])))
+    swaps[4].start()
+    steps(1, 2, 3)
+    swaps[4].wait_recv()
+
+    block = 16
+
+    def norm_rows(i, arrived):
+        at = pl.ds(pl.multiple_of(i * block, block), block)
+        total = part[at, :] + arrived[at, :].astype(jnp.float32)
+        factor = lax.rsqrt(jnp.mean(total * total, axis=1, keepdims=True) + epsilon_norm)
+        return at, factor, total * factor
+
+    def attn_norm(i):
+        at, factor, normed = norm_rows(i, part_in)
+        ahat[at, :] = normed
+        fac_ref[2, at, :] = jnp.broadcast_to(factor, (block, HEAD_DIM))
+        middle = x[at, :].astype(jnp.float32) + normed * gain_ref[2:3, :]
+        mid[at, :] = middle
+        mb[at, :] = middle.astype(jnp.bfloat16)
+
+    loop(length // block, attn_norm)
+    swaps[4].wait_send()
+    save(ahat, ahat_out)
+    save(mb, mb_out)
+    steps(1, 3, 4)
+    complete(1)
+
+    def gate_tile(j, w):
+        gate[:, pl.ds(pl.multiple_of(j * tile, tile), tile)] = nn_dot(mb[...], w[...])
+
+    width = gate.shape[1]
+    stream.cols(1, 0, width // tile, gate_tile)
+    steps(2, 0, 1)
+    begin(3)
+    steps(2, 1, 4)
+    complete(2)
+
+    tall = 64
+
+    def up_tile(j, w):
+        up[...] = nn_dot(mb[...], w[...])
+        view = pl.ds(pl.multiple_of(j * tile, tile), tile)
+
+        def some(i):
+            at = pl.ds(pl.multiple_of(i * tall, tall), tall)
+            g = gate[at, view]
+            u = up[at, :]
+            sig = 1.0 / (1.0 + jnp.exp(-g))
+            act = g * sig
+            silu[at, view] = act.astype(jnp.bfloat16)
+            hid[at, view] = (act * u).astype(jnp.bfloat16)
+            slope[at, view] = (u * sig * (1.0 + g * (1.0 - sig))).astype(jnp.bfloat16)
+
+        loop(length // tall, some)
+
+    stream.cols(2, 0, width // tile, up_tile)
+    save(silu, silu_out)
+    save(slope, slope_out)
+    save(hid, hid_out)
+
+    turn = [0]
+
+    def down(k, slot):
+        stream.row_copy(3, k, slot, 0, width).wait()
+        split(k, chunk, nt_dot(hid[...], wrow[slot]))
+        sum_copy(k, chunk).start()
+
+    def fetch(k):
+        slot = turn[0] % 2
+        turn[0] += 1
+        stream.row_copy(3, k, slot, 0, width).start()
+        return slot
+
+    chunks = D // chunk
+    if chunks == n:
+        own_shared(3)
+        queue = [(ring.chip(0), fetch(ring.chip(0)))]
+
+        def drain():
+            while queue:
+                down(*queue.pop(0))
+
+        for d in range(h):
+            step(3, d)
+            drain()
+            shared(3, d, d + 1)
+            for way in (0, 1):
+                if d < h - 1 or way == 0:
+                    k = ring.chip(-1 - d if way == 0 else 1 + d)
+                    queue.append((k, fetch(k)))
+        drain()
+    else:
+        steps(3, 0, 4)
+        complete(3)
+        for k in range(chunks):
+            down(k, fetch(k))
+
+    def sums(i):
+        sum_copy(i, chunk).wait()
+
+    loop(chunks, sums)
+    load[1].wait()
+    swaps[1].wait_recv()
+    gffn_ref[...] = jnp.zeros_like(gffn_ref)
+    gain = gain_ref[3:4, :]
+
+    def ffn_norm(i):
+        at, factor, normed = norm_rows(i, down_in)
+        y = cot[at, :].astype(jnp.float32)
+
+        @pl.when(i < own_rows // block)
+        def _():
+            out_ref[at, :] = (mid[at, :] + normed * gain).astype(jnp.bfloat16)
+            gffn_ref[0:1, :] += jnp.sum(y * normed, axis=0, keepdims=True)
+
+        scaled = y * gain
+        df[at, :] = (
+            factor * (scaled - normed * jnp.mean(scaled * normed, axis=1, keepdims=True))
+        ).astype(jnp.bfloat16)
+
+    loop(length // block, ffn_norm)
+    save(df, df_out)
+
+    for i in (0, 1):
+        swaps[i].wait_send()
     for w in range(count):
-        if w + 1 < count:
-            begin(w + 1)
-
-        def step(d, carry):
+        def sent(d):
             for way in (0, 1):
-                arrival(w, way, d, None).wait_recv()
-                hop(w, way, d + 1, None).start()
-                share(w, way, d, None).start()
-            return carry
-
-        if h - 2 <= 4:
-            for d in range(h - 2):
-                step(d, 0)
-        else:
-            lax.fori_loop(0, h - 2, step, 0)
-        for d in (h - 2, h - 1):
-            for way in (0, 1):
-                arrival(w, way, d, piece_of(d, way)).wait_recv()
-                if d == h - 2:
-                    hop(w, way, h - 1, way).start()
-                share(w, way, d, piece_of(d, way)).start()
-
-        def finish(d, carry):
-            for way in (0, 1):
-                hop(w, way, d, None).wait_send()
-                share(w, way, d, None).wait_send()
-                share_in(w, way, d, None).wait_recv()
-            return carry
-
-        if h - 1 <= 4:
-            for d in range(h - 1):
-                finish(d, 0)
-        else:
-            lax.fori_loop(0, h - 1, finish, 0)
-        for way in (0, 1):
-            hop(w, way, h - 1, way).wait_send()
-            share(w, way, h - 1, way).wait_send()
-            share_in(w, way, h - 1, way).wait_recv()
-        first, second = own(w)
-        first.wait_send()
-        remote(
-            g_ref.at[w, ring.mate[0]],
-            g_ref.at[w, ring.mate[0]],
-            osend.at[w],
-            orecv.at[w],
-            ring.mate,
-        ).wait_recv()
-        second.wait()
-
-
-def gather_weights(shards, n):
+                hop(w, way, d).wait_send()
+                share(w, way, d, ring.c).wait_send()
+
+        repeat(0, h - 1, sent)
+        sent(h - 1)
+        own_mate(w).wait_send()
+    for copy in saves:
+        copy.wait()
+
+
+def forward(shards, tokens, cotangent, gains, cosine, sine, bias, n):
     count, rows, width = shards.shape
+    own_rows, D = tokens.shape
+    length = 2 * own_rows
+    local = width // 4
+    bf, f32 = jnp.bfloat16, jnp.float32
     dma = pltpu.SemaphoreType.DMA
+    vm = pltpu.VMEM
+    anywhere = pl.BlockSpec(memory_space=pl.ANY)
+    inside = pl.BlockSpec(memory_space=pltpu.VMEM)
+    struct = jax.ShapeDtypeStruct
+    chunk = 256
+    saved = [
+        struct((length, D), bf),
+        struct((length, 2 * local), f32),
+        struct((length, local), bf),
+        struct((length, local), bf),
+        struct((length, local), bf),
+        struct((length, local), bf),
+        struct((length, D), f32),
+        struct((length, D), bf),
+        struct((length, width), bf),
+        struct((length, width), bf),
+        struct((length, width), bf),
+        struct((length, D), bf),
+    ]
     return pl.pallas_call(
-        functools.partial(gather_kernel, n),
-        out_shape=jax.ShapeDtypeStruct((count, 2 * n, rows, width), shards.dtype),
-        in_specs=[pl.BlockSpec(memory_space=pl.ANY)],
-        out_specs=pl.BlockSpec(memory_space=pl.ANY),
+        functools.partial(forward_kernel, n),
+        out_shape=[struct((count, D, width), bf), struct((own_rows, D), bf)]
+        + saved
+        + [struct((3, length, HEAD_DIM), f32), struct((8, D), f32)],
+        in_specs=[anywhere] * 3 + [inside] * 4,
+        out_specs=[anywhere, inside] + [anywhere] * 12 + [inside] * 2,
         scratch_shapes=[
+            vm((length, D), bf),
+            vm((length, D), bf),
+            vm((length, 2 * local), f32),
+            vm((length, local), bf),
+            vm((length, local), bf),
+            vm((length, local), bf),
+            vm((length, local), bf),
+            vm((length, HEAD_DIM), f32),
+            vm((length, HEAD_DIM), f32),
+            vm((length, D), f32),
+            vm((length, D), bf),
+            vm((length, D), bf),
+            vm((length, D), bf),
+            vm((length, D), f32),
+            vm((length, D), f32),
+            vm((length, D), bf),
+            vm((length, width), f32),
+            vm((length, 512), f32),
+            vm((length, width), bf),
+            vm((length, width), bf),
+            vm((length, width), bf),
+            vm((length, D), bf),
+            vm((2, D, 512), bf),
+            vm((2, chunk, width), bf),
             dma((count, 2, 4)),
             dma((count, 2, 4)),
             dma((count, 2, 4)),
             dma((count, 2, 4)),
             dma((count,)),
             dma((count,)),
-            dma((count,)),
+            dma((count + 2,)),
+            dma((2,)),
+            dma((5,)),
+            dma((5,)),
+            dma((D // chunk,)),
+            dma((D // chunk,)),
+            dma((12,)),
         ],
-        compiler_params=pltpu.CompilerParams(collective_id=0, has_side_effects=True),
-        name="gather_weights",
-    )(shards)
+        compiler_params=pltpu.CompilerParams(
+            collective_id=0, has_side_effects=True, vmem_limit_bytes=60 * 1024 * 1024
+        ),
+        name="forward",
+    )(shards, tokens, cotangent, gains, cosine, sine, bias)
 
 
 def scatter_kernel(
@@ -563,89 +989,70 @@
             w_down.T,
         ]
     )
-    gathered = both(tokens)
     gains = lax.all_gather(
         jnp.stack([gain_query, gain_key, gain_attn, gain_ffn]), "fsdp", axis=1, tiled=True
     ).astype(jnp.float32)
-    weights = gather_weights(shards, n)
     D = gains.shape[1]
-    weights = weights.reshape(4, D, shards.shape[2])
-    query_full = weights[0, :, :width]
-    key_full = weights[0, :, width : 2 * width]
-    value_full = weights[0, :, 2 * width : 3 * width]
-    out_t = weights[0, :, 3 * width :]
-    gate_full, up_full, down_t = weights[1], weights[2], weights[3]
-
     rank = lax.axis_index("tensor")
     heads_here = width // HEAD_DIM
     start_col = rank * width
-    gain_query_here = lax.dynamic_slice_in_dim(gains[0], start_col, width)
-    gain_key_here = lax.dynamic_slice_in_dim(gains[1], start_col, width)
-    attn_gain_f = gains[2]
-    ffn_gain_f = gains[3]
-    length = gathered.shape[0]
-    rows = length // 2
+    rows = tokens.shape[0]
+    length = 2 * rows
     segment_row = segment_ids[0]
 
     def arrange(row):
-        flat = lax.dynamic_slice_in_dim(jnp.concatenate([row, row]), rank * rows, length)
-        return flat
+        return lax.dynamic_slice_in_dim(jnp.concatenate([row, row]), rank * rows, length)
 
     indices = arrange(jnp.arange(length, dtype=jnp.int32))
     positions = arrange(doc_positions(segment_row))
     segments = arrange(segment_row)
     cosine, sine_table = rope_tables(positions)
     allowed = (segments[:, None] == segments[None, :]) & (indices[:, None] >= indices[None, :])
-
-    queries = product(gathered, query_full)
-    key_rows = product(gathered, key_full)
-    values = product(gathered, value_full).astype(jnp.bfloat16)
-    squares = jnp.stack([jnp.sum(queries * queries, axis=1), jnp.sum(key_rows * key_rows, axis=1)])
-    squares = squares + jnp.roll(lax.ppermute(squares, "tensor", SWAP), rows, axis=1)
-    query_factor = lax.rsqrt(squares[0] / D + epsilon_norm)[:, None]
-    key_factor = lax.rsqrt(squares[1] / D + epsilon_norm)[:, None]
-    query_hat = queries * query_factor
-    key_hat = key_rows * key_factor
-    queries_r = rotate(
-        (query_hat * gain_query_here).reshape(length, heads_here, HEAD_DIM), cosine, sine_table
-    ).astype(jnp.bfloat16)
-    keys_r = rotate(
-        (key_hat * gain_key_here).reshape(length, heads_here, HEAD_DIM), cosine, sine_table
-    ).astype(jnp.bfloat16)
+    bias = jnp.where(allowed, 0.0, masked_score).astype(jnp.float32)
+    (
+        weights,
+        layer_out,
+        gathered,
+        qk_hat,
+        queries_r,
+        keys_r,
+        values,
+        attended,
+        attn_hat,
+        middle_all,
+        silu_gate,
+        slope_gate,
+        hidden,
+        grad_down_all,
+        factors,
+        ffn_gain_grad,
+    ) = forward(
+        shards,
+        tokens,
+        cotangent,
+        jnp.concatenate([gains, jnp.zeros_like(gains)]),
+        jnp.concatenate([cosine, cosine], axis=1),
+        jnp.concatenate([-sine_table, sine_table], axis=1),
+        bias,
+        n,
+    )
+    out_t = weights[0, :, 3 * width :]
+    gate_full, up_full, down_t = weights[1], weights[2], weights[3]
+    gain_query_here = lax.dynamic_slice_in_dim(gains[0], start_col, width)
+    gain_key_here = lax.dynamic_slice_in_dim(gains[1], start_col, width)
+    attn_gain_f = gains[2]
+    ffn_gain_grad = ffn_gain_grad[0]
+    query_hat, key_hat = qk_hat[:, :width], qk_hat[:, width:]
+    query_factor, key_factor = factors[0, :, :1], factors[1, :, :1]
+    attn_hat = attn_hat[:rows]
+    attn_factor = factors[2, :rows, :1]
+    queries_r = queries_r.reshape(length, heads_here, HEAD_DIM)
+    keys_r = keys_r.reshape(length, heads_here, HEAD_DIM)
     values_r = values.reshape(length, heads_here, HEAD_DIM)
-    scores = attention_scores(queries_r, keys_r, allowed)
-    top_score = jnp.max(scores, axis=-1, keepdims=True)
-    log_total = top_score + jnp.log(jnp.sum(jnp.exp(scores - top_score), axis=-1, keepdims=True))
-    attn_probs = jnp.exp(scores - log_total).astype(jnp.bfloat16)
-    attended = (
-        jnp.einsum("hqk,khd->qhd", attn_probs, values_r, preferred_element_type=jnp.float32)
-        .astype(jnp.bfloat16)
-        .reshape(length, width)
-    )
-    attn_rows = reduce_rows(product_t(attended, out_t))
-    attn_factor = lax.rsqrt(jnp.mean(attn_rows * attn_rows, axis=1) + epsilon_norm)[:, None]
-    attn_hat = attn_rows * attn_factor
-    middle = tokens.astype(jnp.float32) + attn_hat * attn_gain_f
-    middle_all = both(middle.astype(jnp.bfloat16))
-    gate_pre = product(middle_all, gate_full)
-    up_proj = product(middle_all, up_full)
-    sigmoid_gate = jax.nn.sigmoid(gate_pre)
-    silu_gate = gate_pre * sigmoid_gate
-    hidden = (silu_gate * up_proj).astype(jnp.bfloat16)
-    down_rows = reduce_rows(product_t(hidden, down_t))
-    down_factor = lax.rsqrt(jnp.mean(down_rows * down_rows, axis=1) + epsilon_norm)[:, None]
-    down_hat = down_rows * down_factor
-    layer_out = (middle + down_hat * ffn_gain_f).astype(jnp.bfloat16)
-
     grad_out = cotangent.astype(jnp.float32)
-    ffn_gain_grad = jnp.sum(grad_out * down_hat, axis=0)
-    grad_down = norm_back(grad_out, down_hat, down_factor, ffn_gain_f).astype(jnp.bfloat16)
-    grad_down_all = both(grad_down)
     grad_hidden = product(grad_down_all, down_t)
-    grad_gate = (
-        grad_hidden * up_proj * sigmoid_gate * (1.0 + gate_pre * (1.0 - sigmoid_gate))
-    ).astype(jnp.bfloat16)
-    grad_up = (grad_hidden * silu_gate).astype(jnp.bfloat16)
+    grad_gate = (grad_hidden * slope_gate.astype(jnp.float32)).astype(jnp.bfloat16)
+    grad_up = (grad_hidden * silu_gate.astype(jnp.float32)).astype(jnp.bfloat16)
     grad_middle = grad_out + reduce_rows(
         product_t(grad_gate, gate_full) + product_t(grad_up, up_full)
     )
@@ -655,7 +1062,7 @@
     grad_attended = (
         product(grad_attn_all, out_t).astype(jnp.bfloat16).reshape(length, heads_here, HEAD_DIM)
     )
-    probs_again = jnp.exp(attention_scores(queries_r, keys_r, allowed) - log_total)
+    probs_again = jax.nn.softmax(attention_scores(queries_r, keys_r, allowed), axis=-1)
     grad_values = jnp.einsum(
         "hqk,qhd->khd",
         probs_again.astype(jnp.bfloat16),

time: 1130 us -> 1020 us (0.903)
  waiting for transfers between devices: 62.3 us -> 0.01 us
  matrix products: 131 us -> 76.2 us
  Pallas kernels: 684 us -> 738 us
  local copies, waits for them, and re-layouts: 109 us -> 72.6 us
    pallas_call x1, Pallas kernels: 349 us -> 403 us  [forward(): pl.pallas_call(functools.partial(forward_kernel, n), out_shape=[struct((c...]
    dot_general x7 -> x2, matrix products: 61.6 us -> 18 us  [product(): return jnp.dot(left, right, preferred_element_type=jnp.float32)]
    ppermute x4 -> x2, waiting for transfers between devices: 42.3 us -> 0.01 us  [reduce_rows(): other = lax.ppermute(part[rows:].astype(jnp.bfloat16), 'tensor', SWAP)]
    slice x5 -> x4, local copies, waits for them, and re-layouts: 33.8 us -> 3.06 us  [the longest x1 1.19 us: body(): query_factor, key_factor = (factors[0, :, :1], factors[1, :, :1])]
    ppermute x4 -> x1, waiting for transfers between devices: 19.9 us -> 0.01 us  [both(): return jnp.concatenate([own, lax.ppermute(own, 'tensor', SWAP)], axis=0)]
    unnamed x151 -> x54, local copies, waits for them, and re-layouts: 29.8 us -> 16.7 us
    pallas_call x0 -> x4, local copies, waits for them, and re-layouts: none -> 11.4 us  [forward(): pl.pallas_call(functools.partial(forward_kernel, n), out_shape=[struct((c...]
    dot_general x5 -> x3, matrix products: 54.9 us -> 43.7 us  [product_t(): lax.dot_general(left, right, (((1,), (1,)), ((), ())), preferred_element_...]
  transfers between devices with their start and end apart: 10 -> 4, of which waited for: 5 -> 0; matrix products, arithmetic and copies ran while one was open for 9% -> 7% of each run, Pallas kernels for 61% -> 33%
where the time goes in v2:
time: 1020 us; the launch traced here: 1010 us
  Pallas kernels  738 us (72%)
  matrix products  76.2 us (7%)
  local copies, waits for them, and re-layouts  72.6 us (7%)
  blocking collectives  61.9 us (6%)
  other arithmetic  54.8 us (5%)
    pallas_call x1, Pallas kernels, forward(): pl.pallas_call(functools.partial(forward_kernel, n), out_shape=[struct((c...  403 us
    pallas_call x1, Pallas kernels, scatter_gradients(): pl.pallas_call(functools.partial(scatter_kernel, n), out_shape=jax.ShapeD...  335 us
    dot_general x3, matrix products, product_t(): lax.dot_general(left, right, (((1,), (1,)), ((), ())), preferred_element_...  43.7 us
    psum x1, blocking collectives, body(): gain_sums = lax.psum(gain_parts, ('fsdp', 'tensor'))  38.9 us
    all_gather x1, blocking collectives, body(): lax.all_gather(jnp.stack([gain_query, gain_key, gain_attn, gain_ffn]), 'f...  23.1 us
  transfers between devices with their start and end apart: 4, of which 0 were waited for; matrix products, arithmetic and copies ran while one was open for 7% of the time, Pallas kernels for 33%

profile of v2, /device:TPU:0, one launch (start us, length us, event | category | flops | bytes accessed | tf_op | source)
XLA Modules:
  0.0 1011.2 jit_solution(1503914437738042314)
XLA Ops:
  4.0 23.1 %all_gather.3 = bf16[4,2048]{1,0:T(4,128)(2,1)S(1)} all-gather(bf16[4,128]{1,0:T(4,128)(2,1)S(1)} %pad_maximum_fusion.11), channel_id=1, replica_groups=mesh['fsdp'=16,'tensor'=2] {'fsdp'}, dimensions={1}, use_global_device_ids=true | all-gather | bytes 17408 | tf_op jit(solution)/shard_map/all_gather | solution.py:992
  34.0 3.4 pad_maximum_fusion.2.w_ref
  37.4 403.4 %forward.1 = (bf16[4,2048,4096]{2,1,0:T(8,128)(2,1)}, bf16[192,2048]{1,0:T(8,128)(2,1)}, bf16[384,2048]{1,0:T(8,128)(2,1)}, f32[384,2048]{1,0:T(8,128)}, bf16[38...) custom-call(bf16[4,128,4096]{2,1,0:T(8,128)(2,1)} %pad_maximum_fusio, ...), custom_call_target="tpu_custom_call" | custom-call | tf_op jit(solution)/shard_map/forward/pallas_call | solution.py:580
  440.9 12.7 %fusion.5 = f32[384,4096]{1,0:T(8,128)} fusion(bf16[384,2048]{1,0:T(8,128)(2,1)} %get-tuple-element.30, bf16[4,2048,4096]{2,1,0:T(8,128)(2,1)} %get-tuple-element.31), kind=kOutput, calls=%fused_computation.5 | convolution fusion | flops 6442450944 | bytes 24641536 | tf_op jit(solution)/shard_map/dot_general | solution.py:957
  453.5 15.4 %fusion.1 = f32[384,2048]{0,1:T(8,128)} fusion(bf16[4,2048,4096]{2,1,0:T(8,128)(2,1)} %get-tuple-element.31, f32[384,4096]{1,0:T(8,128)} %fusion.5, bf16[384,4096]{1,0:T(8,128)(2,1)S(1)} %copy-done.5), kind=kOutput, calls=%fused_computation.1 | convolution fusion | flops 6447169536 | bytes 29360128 | tf_op jit(solution)/shard_map/dot_general | solution.py:961
  469.0 16.9 %fusion.17 = f32[384,2048]{0,1:T(8,128)} fusion(f32[384,2048]{0,1:T(8,128)} %fusion.1, bf16[4,2048,4096]{2,1,0:T(8,128)(2,1)} %get-tuple-element.31, f32[384,4096]{1,0:T(8,128)} %fusion.5, bf16[384,4096]{1,0:T(8,128)(2,1)} %get-tuple-element.32), kind=kOutput, calls=%fused_computation.27 | convolution fusion | flops 6447955968 | bytes 32505856 | tf_op jit(solution)/shard_map/dot_general | solution.py:961
  490.1 9.4 fusion.51
  500.9 2.6 copy.150
  503.5 3.6 copy.132
  510.3 3.5 multiply_reduce_fusion.1
  521.7 2.6 copy.152
  524.3 2.6 copy.151
  529.0 5.2 fusion.55
  534.2 2.6 copy.134
  536.8 5.3 fusion.34
  544.4 4.4 fusion.31
  548.8 3.3 multiply_reduce_fusion
  560.4 3.0 copy.161
  565.8 3.0 copy.162
  568.8 3.5 multiply_reduce_fusion.4
  574.0 38.9 %psum.7 = f32[4,2048]{1,0:T(4,128)S(1)} all-reduce(f32[4,2048]{1,0:T(4,128)S(1)} %pad_maximum_fusion.9), channel_id=1, replica_groups=mesh['fsdp'=16,'tensor'=2] {'fsdp','tensor'}, use_global_device_ids=true, to_apply=%region_11.12 | all-reduce | flops 8192 | bytes 65536 | tf_op jit(solution)/shard_map/psum | solution.py:1114
  612.9 6.5 pad_maximum_fusion.1.left_hbm
  621.6 3.4 multiply_convert_fusion.5
  625.0 11.4 %fusion.10 = f32[384,2048]{1,0:T(8,128)} fusion(bf16[4,2048,4096]{2,1,0:T(8,128)(2,1)} %get-tuple-element.31, bf16[384,1024]{1,0:T(8,128)(2,1)S(1)} %copy.163, bf16[384,1024]{1,0:T(8,128)(2,1)S(1)} %get-tuple-element.117, bf16[384,1024]{1,0:T(8,128)(2,1)S(1)} %get-tuple-element.116), kind=kOutput, calls=%fused_computation.11 | convolution fusion | flops 4838916096 | bytes 18087936 | tf_op jit(solution)/shard_map/dot_general | solution.py:961
  644.2 5.6 pad_maximum_fusion.right_hbm
  649.7 335.1 %scatter_gradients.1 = f32[4,128,4096]{2,1,0:T(8,128)} custom-call(bf16[4,2048,384]{2,1,0:T(8,128)(2,1)} %pad_maximum_fusion.1.left_hbm, bf16[4,384,4096]{2,1,0:T(8,128)(2,1)} %pad_maximum_fusion.right_hbm), custom_call_target="tpu_custom_call" | custom-call | tf_op jit(solution)/shard_map/scatter_gradients/pallas_call | solution.py:874
  984.8 7.2 slice_bitcast_fusion
  993.2 2.8 copy.164
  996.0 2.7 slice_bitcast_fusion.4
  999.7 2.9 copy.155
  1004.1 3.2 add_add_fusion
  1007.3 2.8 copy.153
  (125 shorter events, 57.9 us)
Async XLA Ops:
  0.6 32.3 %copy-start.13 = (bf16[128,1024]{1,0:T(8,128)(2,1)S(1)}, bf16[128,1024]{1,0:T(8,128)(2,1)}, u32[]{:S(2)}) copy-start(bf16[128,1024]{1,0:T(8,128)(2,1)} %param.18) | copy-start | bytes 786436
  0.7 32.3 %copy-start.14 = (bf16[128,1024]{1,0:T(8,128)(2,1)S(1)}, bf16[128,1024]{1,0:T(8,128)(2,1)}, u32[]{:S(2)}) copy-start(bf16[128,1024]{1,0:T(8,128)(2,1)} %param.17) | copy-start | bytes 786436
  29.6 7.9 copy-start.16
  29.6 7.8 copy-start.18
  440.9 12.7 %copy-start.5 = (bf16[384,4096]{1,0:T(8,128)(2,1)S(1)}, bf16[384,4096]{1,0:T(8,128)(2,1)}, u32[]{:S(2)}) copy-start(bf16[384,4096]{1,0:T(8,128)(2,1)} %get-tuple-element.33) | copy-start | bytes 9437188
  488.5 11.0 %copy-start.8 = (bf16[192,2048]{1,0:T(8,128)(2,1)S(1)}, bf16[192,2048]{1,0:T(8,128)(2,1)}, u32[]{:S(2)}) copy-start(bf16[192,2048]{1,0:T(8,128)(2,1)} %cot_ref.1) | copy-start | bytes 2359300
  488.5 19.6 %collective-permute-start = (bf16[192,2048]{1,0:T(8,128)(2,1)S(1)}, bf16[192,2048]{1,0:T(8,128)(2,1)}, u32[]{:S(2)}, u32[]{:S(2)}) collective-permute-start(bf16[192,2048]{1,0:T(8,128)(2,1)S(1)} %copy.127), channel_id=1, source_target_pairs={{0,1},{1,0},{2,3},{3,2},{4,5},{5,4},{6,7},{7,6},{8,9},{9,8},{10,11... | collective-permute-start | bytes 2359304 | tf_op jit(solution)/shard_map/ppermute | solution.py:909
  510.3 3.6 copy-start
  513.9 2.2 copy-start.17
  513.9 2.1 copy-start.19
  515.5 18.7 %collective-permute-start.1 = (bf16[192,2048]{1,0:T(8,128)(2,1)}, bf16[192,2048]{1,0:T(8,128)(2,1)}, u32[]{:S(2)}, u32[]{:S(2)}) collective-permute-start(bf16[192,2048]{1,0:T(8,128)(2,1)} %copy.133), channel_id=1, source_target_pairs={{0,1},{1,0},{2,3},{3,2},{4,5},{5,4},{6,7},{7,6},{8,9},{9,8},{10,11... | collective-permute-start | bytes 2359304 | tf_op jit(solution)/shard_map/ppermute | solution.py:904
  521.7 7.3 copy-start.15
  544.4 4.4 copy-start.11
  544.4 4.4 copy-start.20
  548.8 3.6 slice-start
  548.8 3.7 slice-start.1
  552.6 1.1 copy-start.7
  553.7 1.1 copy-start.6
  554.8 1.2 copy-start.3
  554.8 3.0 copy-start.12
  572.3 49.0 %collective-permute-start.2 = (f32[2,384]{1,0:T(2,128)S(1)}, f32[2,384]{1,0:T(2,128)S(1)}, u32[]{:S(2)}, u32[]{:S(2)}) collective-permute-start(f32[2,384]{1,0:T(2,128)S(1)} %pad_maximum_fusion.10), channel_id=1, source_target_pairs={{0,1},{1,0},{2,3},{3,2},{4,5},{5,4},{6,7},{7,6},{8,9},{9,8},{10,11... | collective-permute-start | bytes 9224 | tf_op jit(solution)/shard_map/ppermute | solution.py:1096
  625.0 17.6 %copy-start.4 = (bf16[384,4096]{1,0:T(8,128)(2,1)S(1)}, bf16[384,4096]{1,0:T(8,128)(2,1)}, u32[]{:S(2)}) copy-start(bf16[384,4096]{1,0:T(8,128)(2,1)} %get-tuple-element.42) | copy-start | bytes 9437188
  638.8 363.8 %collective-permute-start.3 = (bf16[192,2048]{1,0:T(8,128)(2,1)}, bf16[192,2048]{1,0:T(8,128)(2,1)}, u32[]{:S(2)}, u32[]{:S(2)}) collective-permute-start(bf16[192,2048]{1,0:T(8,128)(2,1)} %slice.267), channel_id=1, source_target_pairs={{0,1},{1,0},{2,3},{3,2},{4,5},{5,4},{6,7},{7,6},{8,9},{9,8},{10,11... | collective-permute-start | bytes 2359304 | tf_op jit(solution)/shard_map/ppermute | solution.py:909
  641.1 2.1 copy-start.1
  641.1 3.1 copy-start.2
  984.8 7.2 copy-start.9
  1007.3 2.8 copy-start.10
